TPU v7x, 128 devices: a whole 4x4x4 slice. The times are simulated.
128 devices in a mesh: heads: 1, cpo: 16 (over z, y), cp: 8 (over x, core).
Axes of the slice: x: 4, y: 4, z: 4, core: 2. Of those that a mesh axis runs over, the one named last changes fastest.
Arguments:
- queries: bfloat16 [2, 1024, 24, 128], P(None, ('cpo', 'cp'), 'heads')
- attn_out: bfloat16 [2, 1024, 24, 128], P(None, ('cpo', 'cp'), 'heads')
- grad_out: bfloat16 [2, 1024, 24, 128], P(None, ('cpo', 'cp'), 'heads')
- log_sum_exp: float32 [2, 1024, 24], P(None, ('cpo', 'cp'), 'heads')
- key_cache: bfloat16 [4096, 8, 128], P(('cpo', 'cp'), 'heads')
- value_cache: bfloat16 [4096, 8, 128], P(('cpo', 'cp'), 'heads')
Outputs:
- output 1: bfloat16 [2, 1024, 24, 128], P(None, ('cpo', 'cp'), 'heads')
- output 2: float32 [4096, 8, 128], P(('cpo', 'cp'), 'heads')
- output 3: float32 [4096, 8, 128], P(('cpo', 'cp'), 'heads')
All inputs are finite; a program needn't handle non-finite values.
Results may differ from a plain program's by a relative error of at most 0.001.
Values are sent between devices in bfloat16 or wider.
A program may use at most 1 GiB of HBM per device.

v0:
```python
import jax
import jax.numpy as jnp
from jax import lax
from jax.sharding import PartitionSpec as P

CP_AXES = ('cpo', 'cp')


def rows_per_step(n_rows, row_width):
    block_rows = n_rows
    while block_rows % 2 == 0 and block_rows * row_width > 4194304:
        block_rows = block_rows // 2
    return block_rows


def make_step(key_part, value_part, key_pos, softmax_scale):
    def block_step(carry_acc, operand):
        acc_key, acc_value = carry_acc
        q_blk, g_blk, stat_blk, row_start = operand
        lse_rows = jnp.transpose(stat_blk[..., 0], (1, 0, 2))
        delta_rows = jnp.transpose(stat_blk[..., 1], (1, 0, 2))
        scores = jnp.einsum('rhgd,khd->hrgk', q_blk, key_part, preferred_element_type=jnp.float32)
        q_pos = row_start + jnp.arange(q_blk.shape[0])
        visible = (key_pos[None, :] <= q_pos[:, None])[None, :, None, :]
        attn_prob = jnp.where(visible, jnp.exp(scores * softmax_scale - lse_rows[..., None]), 0.0)
        acc_value = acc_value + jnp.einsum('hrgk,rhgd->hkd', attn_prob.astype(jnp.bfloat16), g_blk, preferred_element_type=jnp.float32)
        grad_prob = jnp.einsum('rhgd,khd->hrgk', g_blk, value_part, preferred_element_type=jnp.float32)
        grad_scores = (attn_prob * (grad_prob - delta_rows[..., None])).astype(jnp.bfloat16)
        dq_blk = jnp.einsum('hrgk,khd->rhgd', grad_scores, key_part, preferred_element_type=jnp.float32) * softmax_scale
        acc_key = acc_key + softmax_scale * jnp.einsum('hrgk,rhgd->hkd', grad_scores, q_blk, preferred_element_type=jnp.float32)
        return (acc_key, acc_value), dq_blk

    return block_step


def solution(mesh):
    n_dev = mesh.shape['cpo'] * mesh.shape['cp']
    inner_size = mesh.shape['cp']
    row_spec = P(None, CP_AXES, 'heads', None)
    stat_spec = P(None, CP_AXES, 'heads')
    key_spec = P(CP_AXES, 'heads', None)

    def local_grads(queries, attn_out, grad_out, log_sum_exp, key_cache, value_cache):
        n_slices, rows_dev, q_heads, head_dim = queries.shape
        key_rows = key_cache.shape[0]
        kv_heads = key_cache.shape[1]
        group_size = q_heads // kv_heads
        slice_len = rows_dev * n_dev
        prefix_base = key_rows * n_dev - n_slices * slice_len
        softmax_scale = head_dim ** -0.5
        dev_idx = lax.axis_index('cpo') * inner_size + lax.axis_index('cp')
        key_pos = dev_idx * key_rows + jnp.arange(key_rows)
        block_rows = rows_per_step(slice_len, q_heads * key_rows)
        n_blocks = slice_len // block_rows
        blk_shape = (n_blocks, block_rows, kv_heads, group_size)
        row_delta = jnp.sum(grad_out.astype(jnp.float32) * attn_out.astype(jnp.float32), axis=-1)
        row_stats = jnp.stack([log_sum_exp, row_delta], axis=-1)
        block_step = make_step(key_cache, value_cache, key_pos, softmax_scale)
        acc_key = jnp.zeros((kv_heads, key_rows, head_dim), jnp.float32)
        acc_value = jnp.zeros((kv_heads, key_rows, head_dim), jnp.float32)
        dq_list = []
        for slice_idx in reversed(range(n_slices)):
            q_all = lax.all_gather(queries[slice_idx], CP_AXES, axis=0, tiled=True)
            g_all = lax.all_gather(grad_out[slice_idx], CP_AXES, axis=0, tiled=True)
            stat_all = lax.all_gather(row_stats[slice_idx], CP_AXES, axis=0, tiled=True)
            row_starts = prefix_base + slice_idx * slice_len + block_rows * jnp.arange(n_blocks)
            operands = (q_all.reshape(blk_shape + (head_dim,)), g_all.reshape(blk_shape + (head_dim,)), stat_all.reshape(blk_shape + (2,)), row_starts)
            (acc_key, acc_value), dq_blocks = lax.scan(block_step, (acc_key, acc_value), operands)
            dq_part = dq_blocks.reshape(slice_len, q_heads, head_dim)
            dq_list.append(lax.psum_scatter(dq_part, CP_AXES, scatter_dimension=0, tiled=True).astype(jnp.bfloat16))
        grad_query = jnp.stack(dq_list[::-1])
        return grad_query, jnp.transpose(acc_key, (1, 0, 2)), jnp.transpose(acc_value, (1, 0, 2))

    return jax.shard_map(local_grads, mesh=mesh, in_specs=(row_spec, row_spec, row_spec, stat_spec, key_spec, key_spec), out_specs=(row_spec, key_spec, key_spec), check_vma=False)
```

profile of v0, /device:TPU:1, one launch (start us, length us, event | category | flops | bytes accessed | tf_op | source)
XLA Modules:
  0.0 748.9 jit_solution(11495857353521071941)
XLA Ops:
  7.2 1.5 slice_bitcast_fusion.3
  8.8 1.5 slice_bitcast_fusion.2
  10.3 0.7 all-gather.15.cloned.1.call-update
  11.0 0.5 all-gather.17.cloned.1.call-update
  11.6 1.1 multiply_reduce_fusion
  12.7 0.7 fusion.37
  13.4 40.8 %all-gather.1 = f32[1,1024,24,2]{2,1,0,3:T(8,128)S(1)} all-gather(f32[1,8,24,2]{2,1,0,3:T(8,128)S(1)} %get-tuple-element.83), channel_id=3, replica_groups=mesh['heads'=1,'cpo'=16,'cp'=8] {'cpo','cp'}, dimensions={1}, use_global_device_ids=true | all-gather | bytes 198144 | tf_op jit(solution)/shard_map/all_gather | solution.py:65
  54.2 0.3 copy.70
  54.5 0.2 fusion.42
  54.7 0.1 copy.77
  54.8 0.1 copy.72
  54.9 0.7 broadcast_compare_fusion.1
  55.6 28.2 %all-gather.11.cloned.1.call-done = bf16[1,1024,24,128]{3,2,0,1:T(8,128)(2,1)} async-done(((bf16[1,8,24,128]{3,2,0,1:T(8,128)(2,1)}), bf16[1,1024,24,128]{3,2,0,1:T(8,128)(2,1)}) %all-gather.11.cloned.1.call-update) | async-done | bytes 6291472 | tf_op jit(solution)/shard_map/all_gather | solution.py:63
  83.8 6.8 copy.68
  90.6 62.6 %all-gather.13.cloned.1.call-done = bf16[1,1024,24,128]{3,2,0,1:T(8,128)(2,1)} async-done(((bf16[1,8,24,128]{3,2,0,1:T(8,128)(2,1)}), bf16[1,1024,24,128]{3,2,0,1:T(8,128)(2,1)}) %all-gather.13.cloned.1.call-update) | async-done | bytes 6291472 | tf_op jit(solution)/shard_map/all_gather | solution.py:64
  153.2 4.3 copy.74
  157.5 0.3 copy-done.3
  157.8 2.2 fusion.35
  160.1 0.1 copy-done.1
  160.1 2.4 multiply_convert_fusion.1
  162.5 6.0 broadcast_multiply_fusion.1
  168.5 16.4 %copy.79 = f32[1024,24,128]{2,1,0:T(8,128)} copy(f32[1024,24,128]{2,0,1:T(8,128)} %bitcast.92) | data formatting | bytes 25165824 | tf_op jit(solution)/shard_map/reshape | solution.py:69
  184.9 36.7 %all-gather.4 = f32[1,1024,24,2]{2,1,0,3:T(8,128)} all-gather(f32[1,8,24,2]{2,1,0,3:T(8,128)S(1)} %get-tuple-element.84), channel_id=6, replica_groups=mesh['heads'=1,'cpo'=16,'cp'=8] {'cpo','cp'}, dimensions={1}, use_global_device_ids=true | all-gather | bytes 198144 | tf_op jit(solution)/shard_map/all_gather | solution.py:65
  221.6 1.6 copy.83
  223.2 0.2 fusion.43
  223.4 0.1 copy.85
  223.5 0.7 copy.90
  224.2 6.8 copy.81
  231.0 62.3 %all-gather.17.cloned.1.call-done = bf16[1,1024,24,128]{3,2,0,1:T(8,128)(2,1)} async-done(((bf16[1,8,24,128]{3,2,0,1:T(8,128)(2,1)}), bf16[1,1024,24,128]{3,2,0,1:T(8,128)(2,1)}) %all-gather.17.cloned.1.call-update) | async-done | bytes 6291472 | tf_op jit(solution)/shard_map/all_gather | solution.py:64
  293.3 4.3 copy.87
  297.6 0.3 copy-done.4
  297.9 2.2 fusion.32
  300.2 3.2 multiply_convert_fusion
  303.4 6.1 broadcast_multiply_fusion
  309.5 16.4 %copy.92 = f32[1024,24,128]{2,1,0:T(8,128)} copy(f32[1024,24,128]{2,0,1:T(8,128)} %bitcast.93) | data formatting | bytes 25165824 | tf_op jit(solution)/shard_map/reshape | solution.py:69
  326.0 4.5 convolution_bitcast_fusion.1
  330.5 4.0 fusion.22
  334.5 0.7 copy.93
  335.3 1.3 fusion.14
  336.6 0.3 slice-done.3
  336.9 0.9 copy-done.6
  337.8 1.3 fusion.26
  339.1 0.7 copy.94
  339.8 175.7 %reduce-scatter.3.cloned.1.call-done = f32[8,24,128]{2,1,0:T(8,128)} async-done(((f32[1024,24,128]{2,1,0:T(8,128)}), f32[8,24,128]{2,1,0:T(8,128)}) %reduce-scatter.3.cloned.1.call-update) | async-done | bytes 98320 | tf_op jit(solution)/shard_map/reduce_scatter | solution.py:70
  515.5 0.9 convert_bitcast_fusion.1
  516.4 223.7 %reduce-scatter.5.cloned.1.call-done = f32[8,24,128]{2,1,0:T(8,128)} async-done(((f32[1024,24,128]{2,1,0:T(8,128)}), f32[8,24,128]{2,1,0:T(8,128)}) %reduce-scatter.5.cloned.1.call-update) | async-done | bytes 98320 | tf_op jit(solution)/shard_map/reduce_scatter | solution.py:70
  740.0 0.9 convert_bitcast_fusion
  740.9 0.7 pad_maximum_fusion
  (51 shorter events, 0.5 us)
Async XLA Ops:
  7.2 150.4 %copy-start = (bf16[32,8,128]{2,1,0:T(8,128)(2,1)S(1)}, bf16[32,8,128]{2,1,0:T(8,128)(2,1)}, u32[]{:S(2)}) copy-start(bf16[32,8,128]{2,1,0:T(8,128)(2,1)} %param.10) | copy-start | bytes 196612
  7.2 76.7 %all-gather.11.cloned.1.call-start = ((), (), s32[]{:S(2)}) async-start(), calls=%async_computation.4 | async-start | bytes 6340608 | tf_op jit(solution)/shard_map/all_gather | solution.py:63
  8.7 144.5 %all-gather.13.cloned.1.call-start = ((), (), s32[]{:S(2)}) async-start(), calls=%async_computation.5 | async-start | bytes 6340608 | tf_op jit(solution)/shard_map/all_gather | solution.py:64
  10.3 213.9 %all-gather.15.cloned.1.call-start = ((), (), s32[]{:S(2)}) async-start(), calls=%async_computation.6 | async-start | bytes 6340608 | tf_op jit(solution)/shard_map/all_gather | solution.py:63
  11.0 282.3 %all-gather.17.cloned.1.call-start = ((), (), s32[]{:S(2)}) async-start(), calls=%async_computation.7 | async-start | bytes 6340608 | tf_op jit(solution)/shard_map/all_gather | solution.py:64
  11.6 503.9 %reduce-scatter.3.cloned.1.call-start = ((), (), s32[]{:S(2)}) async-start(), calls=%async_computation.2 | async-start | bytes 12681216 | tf_op jit(solution)/shard_map/reduce_scatter | solution.py:70
  55.6 104.4 %copy-start.11 = (pred[1024,32]{0,1:T(8,128)(4,1)}, pred[1024,32]{0,1:T(8,128)(4,1)S(1)}, u32[]{:S(2)}) copy-start(pred[1024,32]{0,1:T(8,128)(4,1)S(1)} %get-tuple-element.85) | copy-start | bytes 98308
  153.2 4.6 copy-start.3
  157.5 2.6 copy-start.1
  157.8 2.3 copy-start.14
  162.5 6.0 copy-start.7
  184.9 555.1 %reduce-scatter.5.cloned.1.call-start = ((), (), s32[]{:S(2)}) async-start(), calls=%async_computation.3 | async-start | bytes 12681216 | tf_op jit(solution)/shard_map/reduce_scatter | solution.py:70
  293.3 4.6 copy-start.4
  297.6 2.6 copy-start.2
  297.9 2.3 copy-start.10
  297.9 2.3 copy-start.13
  300.1 3.3 copy-start.5
  303.4 6.1 copy-start.9
  325.9 4.5 copy-start.8
  325.9 9.3 %slice-start = ((s8[6291456]{0:T(1024)(128)(4,1)}), s8[4194304]{0:T(1024)(128)(4,1)S(1)}, s32[]{:S(2)}) async-start(s8[6291456]{0:T(1024)(128)(4,1)} %bitcast.95), calls=%async_computation.8 | async-start | bytes 8388608
  330.4 4.8 slice-start.1
  330.4 4.8 copy-start.12
  330.5 6.1 slice-start.2
  335.3 1.6 slice-start.3
  335.3 2.5 copy-start.6
Sparse Core Ops, SparseCore 0:
  11.7 72.1 all-gather.10
  87.5 65.6 all-gather.12
  156.9 67.2 all-gather.14
  227.1 66.0 all-gather.16
  298.1 217.3 reduce-scatter.2
  520.3 219.6 reduce-scatter.4
where the time goes:
time: 756 us; the launch traced here: 749 us
  waiting for transfers between devices  554 us (73%)
  blocking collectives  77.5 us (10%)
  local copies, waits for them, and re-layouts  64.5 us (9%)
  matrix products  33.1 us (4%)
  between operations  14.9 us (2%)
    reduce_scatter x2, waiting for transfers between devices, local_grads(): lax.psum_scatter(dq_part, CP_AXES, scatter_dimension=0, tiled=True)  399 us
    all_gather x2, waiting for transfers between devices, local_grads(): g_all = lax.all_gather(grad_out[slice_idx], CP_AXES, axis=0, tiled=True)  125 us
    all_gather x2, blocking collectives, local_grads(): stat_all = lax.all_gather(row_stats[slice_idx], CP_AXES, axis=0, tiled=True)  77.5 us
    reshape x2, local copies, waits for them, and re-layouts, local_grads(): dq_part = dq_blocks.reshape(slice_len, q_heads, head_dim)  32.8 us
    all_gather x2, waiting for transfers between devices, local_grads(): q_all = lax.all_gather(queries[slice_idx], CP_AXES, axis=0, tiled=True)  28.2 us
  transfers between devices with their start and end apart: 6, of which 5 were waited for; matrix products, arithmetic and copies ran while one was open for 13% of the time, Pallas kernels for 0%

commit v1 on v0

v1 whole, which is shorter than its diff:
```python
import jax
import jax.numpy as jnp
from jax import lax
from jax.experimental import pallas as pl
from jax.experimental.pallas import tpu as pltpu
from jax.sharding import PartitionSpec as P

CP_AXES = ('cpo', 'cp')
MESH = pl.DeviceIdType.MESH
LOG2E = 1.4426950408889634

ROW = 8
RING = 4
GRP = 3
TOK = 16
KEYS = 32
DIM = 128
HALF = ROW // 2
QROWS = ROW * GRP * TOK
KROWS = ROW * KEYS
PACK = GRP * TOK
SCALE = DIM ** -0.5
NSEM = 80

NT = (((1,), (1,)), ((), ()))
NN = (((1,), (0,)), ((), ()))
TN = (((0,), (0,)), ((), ()))


def dot(a, b, dims):
    return lax.dot_general(a, b, dims, preferred_element_type=jnp.float32)


def kernel(q_in, o_in, g_in, l_in, k_in, v_in, out_q, out_kv,
           q_vm, o_vm, g_vm, l_vm, k_vm, v_vm, xs, xk, ts, tt,
           pq, pst, pkv, qd, st, kv, ld, rowc, akv, aqt, oq,
           ra_kv, rb_kv, ra_q, rb_q, fq, in_sem, ssem, rsem):
    me = lax.axis_index('cp')
    cpo = lax.axis_index('cpo')
    z, y = cpo // RING, cpo % RING

    def row_dev(j):
        return (0, cpo, j)

    def ring_devs(axis):
        if axis == 'y':
            return [(0, z * RING + (y + d) % RING, me) for d in (1, 3)]
        return [(0, ((z + d) % RING) * RING + y, me) for d in (1, 3)]

    ydev, zdev = ring_devs('y'), ring_devs('z')

    barrier = pltpu.get_barrier_semaphore()
    for j in range(1, ROW):
        pl.semaphore_signal(barrier, inc=1, device_id=row_dev((me + j) % ROW), device_id_type=MESH)
    for dev in ydev + zdev:
        pl.semaphore_signal(barrier, inc=1, device_id=dev, device_id_type=MESH)

    loads = [pltpu.make_async_copy(src, dst, in_sem.at[i]) for i, (src, dst) in enumerate(
        ((g_in, g_vm), (o_in, o_vm), (q_in, q_vm), (l_in, l_vm), (k_in, k_vm), (v_in, v_vm)))]
    for ld_copy in loads:
        ld_copy.start()

    counter = [0]

    def take(n):
        first = counter[0]
        counter[0] += n
        assert counter[0] <= NSEM
        return first

    def remote(src, dst, send_i, recv_i, dev):
        return pltpu.make_async_remote_copy(
            src_ref=src, dst_ref=dst, send_sem=ssem.at[send_i], recv_sem=rsem.at[recv_i],
            device_id=dev, device_id_type=MESH)

    sent = []

    loads[0].wait()
    loads[1].wait()
    gf = g_vm[...].reshape(TOK, ROW * GRP, DIM).astype(jnp.float32)
    xs[...] = gf
    of = o_vm[...].reshape(TOK, ROW * GRP, DIM).astype(jnp.float32)
    delta = jnp.sum(gf * of, axis=-1)
    ts[...] = jnp.zeros_like(ts)
    loads[3].wait()
    ts[pl.ds(0, TOK), pl.ds(0, ROW * GRP)] = l_vm[...].reshape(TOK, ROW * GRP)
    ts[pl.ds(TOK, TOK), pl.ds(0, ROW * GRP)] = delta
    for h in range(ROW):
        for g in range(GRP):
            pq[h, GRP + g] = xs[:, h * GRP + g, :].astype(jnp.bfloat16)
    loads[2].wait()
    xs[...] = q_vm[...].reshape(TOK, ROW * GRP, DIM).astype(jnp.float32)
    for h in range(ROW):
        for g in range(GRP):
            pq[h, g] = xs[:, h * GRP + g, :].astype(jnp.bfloat16)
    tt[...] = ts[...].T
    lane = lax.broadcasted_iota(jnp.int32, (ROW, DIM), 1)
    for which in range(2):
        packed = jnp.zeros((ROW, DIM), jnp.float32)
        for g in range(GRP):
            part = tt[pl.ds(g, ROW, stride=GRP), :]
            shift = (g * TOK - which * TOK) % DIM
            if shift:
                part = pltpu.roll(part, shift, 1)
            packed = jnp.where((lane >= g * TOK) & (lane < (g + 1) * TOK), part, packed)
        pst[:, which, :] = pltpu.roll(packed, (PACK * me) % DIM, 1)

    pl.semaphore_wait(barrier, ROW - 1 + 4)

    def row_send(src, dst, base):
        for j in (4, 5, 2, 3, 6, 7, 1):
            d = (me + j) % ROW
            remote(src.at[d], dst.at[0, me], base + d, base + me, row_dev(d)).start()

    def row_wait(buf, base, s):
        @pl.when(me != s)
        def _():
            remote(buf.at[0, s], buf.at[0, s], base + s, base + s, row_dev(s)).wait_recv()

    def row_wait_send(src, dst, base):
        for j in range(1, ROW):
            d = (me + j) % ROW
            remote(src.at[d], dst.at[0, me], base + d, base + me, row_dev(d)).wait_send()

    xq, xst, xkv = take(ROW), take(ROW), take(ROW)
    row_send(pq, qd, xq)
    row_send(pst, st, xst)
    qd[0, me] = pq[me]
    st[0, me] = pst[me]

    loads[4].wait()
    xk[...] = k_vm[...].astype(jnp.float32)
    for h in range(ROW):
        pkv[h, 0] = xk[:, h, :].astype(jnp.bfloat16)
    loads[5].wait()
    xk[...] = v_vm[...].astype(jnp.float32)
    for h in range(ROW):
        pkv[h, 1] = xk[:, h, :].astype(jnp.bfloat16)
    row_send(pkv, kv, xkv)
    kv[0, me] = pkv[me]

    r_id = lax.broadcasted_iota(jnp.int32, (1, QROWS), 1)
    rowc[...] = (((r_id >> 3) & 1) * 1024 + ((r_id * 1366) >> 16) * 8 + (r_id & 7)) + (2048 + z * 256 - y * 256)
    akv[...] = jnp.zeros_like(akv)
    aqt[...] = jnp.zeros_like(aqt)

    class Gather:
        def __init__(self, buf, devs):
            self.buf, self.devs = buf, devs
            self.near = take(4)
            self.far = take(2)

        def part(self, slot, half):
            return self.buf.at[slot, pl.ds(half * HALF, HALF)]

        def near_copy(self, slot, half):
            i = self.near + (slot - 1) * 2 + half
            return remote(self.part(0, half), self.part(slot, half), i, i, self.devs[slot - 1])

        def far_copy(self, half):
            i = self.far + half
            return remote(self.part(1 + half, half), self.part(3, half), i, i, self.devs[half])

        def send(self, half):
            for slot in (1, 2):
                self.near_copy(slot, half).start()
                sent.append((self.near_copy, slot, half))

        def wait(self, slot, half):
            self.near_copy(slot, half).wait_recv()

        def forward(self, half):
            self.wait(1 + half, half)
            self.far_copy(half).start()
            sent.append((self.far_copy, half))

        def wait_far(self):
            for half in (0, 1):
                self.far_copy(half).wait_recv()

    agq, agst, agkv = Gather(qd, ydev), Gather(st, ydev), Gather(kv, zdev)
    for half in (0, 1):
        for s in range(half * HALF, (half + 1) * HALF):
            row_wait(qd, xq, s)
            row_wait(st, xst, s)
        agq.send(half)
        agst.send(half)
    for half in (0, 1):
        for s in range(half * HALF, (half + 1) * HALF):
            row_wait(kv, xkv, s)
        agkv.send(half)

    src_id = lax.broadcasted_iota(jnp.int32, (ROW, DIM), 0)

    def assemble(slot):
        for which in range(2):
            rows = st[slot, :, which, :]
            for k in range(QROWS // DIM):
                mine = (((lane + k * DIM) * 1366) >> 16) == src_id
                line = jnp.sum(jnp.where(mine, rows, 0.0), axis=0, keepdims=True)
                ld[slot, pl.ds(which, 1), pl.ds(k * DIM, DIM)] = line * LOG2E if which == 0 else line

    class Scatter:
        def __init__(self, acc, ra, rb, devs):
            self.acc, self.ra, self.rb, self.devs = acc, ra, rb, devs
            self.first = take(2)
            self.second = take(4)

        def part(self, slot, half):
            return self.acc.at[slot, pl.ds(half * HALF, HALF)]

        def far_copy(self, half):
            i = self.first + half
            return remote(self.part(3, half), self.ra.at[half], i, i, self.devs[half])

        def near_copy(self, side, half):
            i = self.second + side * 2 + half
            return remote(self.part(2 - side, half), self.rb.at[side, pl.ds(half * HALF, HALF)], i, i, self.devs[side])

        def send_far(self):
            for half in (0, 1):
                self.far_copy(half).start()
                sent.append((self.far_copy, half))

        def send_early(self, side):
            self.near_copy(side, 1 - side).start()
            sent.append((self.near_copy, side, 1 - side))

        def send_late(self, side):
            self.far_copy(side).wait_recv()
            part = pl.ds(side * HALF, HALF)
            self.acc[2 - side, part] = self.acc[2 - side, part] + self.ra[side]
            self.near_copy(side, side).start()
            sent.append((self.near_copy, side, side))

        def total(self, half):
            for side in (0, 1):
                self.near_copy(side, half).wait_recv()
            part = pl.ds(half * HALF, HALF)
            return self.acc[0, part] + self.rb[0, part] + self.rb[1, part]

    rskv, rsq = Scatter(akv, ra_kv, rb_kv, zdev), Scatter(oq, ra_q, rb_q, ydev)

    key_row = lax.broadcasted_iota(jnp.int32, (KROWS, QROWS), 0)

    def offset(slot):
        return jnp.where(slot == 1, 3, jnp.where(slot == 2, 1, jnp.where(slot == 3, 2, 0)))

    def block(qs, ks):
        yq = (y + offset(qs)) % RING
        zk = (z + offset(ks)) % RING
        q = qd[qs, :, pl.ds(0, GRP)].reshape(QROWS, DIM)
        g = qd[qs, :, pl.ds(GRP, GRP)].reshape(QROWS, DIM)
        k = kv[ks, :, 0].reshape(KROWS, DIM)
        v = kv[ks, :, 1].reshape(KROWS, DIM)
        lse = ld[qs, pl.ds(0, 1), :]
        dlt = ld[qs, pl.ds(1, 1), :]
        thr = rowc[...] + (yq * 64 - zk * 1024)
        s_t = dot(k, q, NT)
        p_t = jnp.where(key_row <= thr, jnp.exp2(s_t * (SCALE * LOG2E) - lse), 0.0)
        dp_t = dot(v, g, NT)
        ds_t = (p_t * (dp_t - dlt)).astype(jnp.bfloat16)
        akv[ks, :, 1] = akv[ks, :, 1] + dot(p_t.astype(jnp.bfloat16), g, NN).reshape(ROW, KEYS, DIM)
        akv[ks, :, 0] = akv[ks, :, 0] + dot(ds_t, q, NN).reshape(ROW, KEYS, DIM)
        aqt[qs] = aqt[qs] + dot(k, ds_t, TN)

    def finish_q(slot):
        oq[slot] = aqt[slot].T.reshape(ROW, PACK, DIM)

    def before_0():
        assemble(0)

    def before_1():
        for half in (0, 1):
            agq.forward(half)
            agst.forward(half)
        for half in (0, 1):
            agkv.forward(half)
        agkv.wait(1, 1)

    def before_2():
        agkv.wait(2, 0)

    def before_3():
        agq.wait(1, 1)
        agst.wait(1, 1)
        assemble(1)

    def before_6():
        agq.wait(2, 0)
        agst.wait(2, 0)
        assemble(2)

    def before_9():
        agkv.wait_far()

    def before_12():
        agq.wait_far()
        agst.wait_far()
        assemble(3)

    def after_10():
        finish_q(1)
        rsq.send_early(1)

    def after_11():
        finish_q(2)
        rsq.send_early(0)

    def after_15():
        finish_q(3)
        rsq.send_far()

    before = {0: before_0, 1: before_1, 2: before_2, 3: before_3, 6: before_6, 9: before_9, 12: before_12}
    after = {9: lambda: finish_q(0), 10: after_10, 11: after_11, 12: rskv.send_far,
             13: lambda: rskv.send_early(1), 14: lambda: rskv.send_early(0), 15: after_15}

    def step(i, carry):
        for n, act in before.items():
            pl.when(i == n)(act)
        qs = jnp.where(i < 9, i // 3, jnp.where(i < 12, i - 9, 3))
        late = jnp.where(i == 12, 3, jnp.where(i == 15, 0, i - 12))
        ks = jnp.where(i < 9, i % 3, jnp.where(i < 12, 3, late))
        block(qs, ks)
        for n, act in after.items():
            pl.when(i == n)(act)
        return carry

    lax.fori_loop(0, 16, step, 0)

    rskv.send_late(1)
    rskv.send_late(0)
    rsq.send_late(1)
    rsq.send_late(0)

    fkv_i, fq_i = take(ROW), take(ROW)

    def give(src, dst, base, half):
        for s in range(half * HALF, (half + 1) * HALF):
            @pl.when(me != s)
            def _():
                remote(src(s), dst.at[me], base + s, base + me, row_dev(s)).start()

    for half in (0, 1):
        tot = rskv.total(half)
        part = pl.ds(half * HALF, HALF)
        akv[0, part, 0] = tot[:, 0] * SCALE
        akv[0, part, 1] = tot[:, 1]
        give(lambda s: akv.at[0, s], out_kv, fkv_i, half)
    out_kv[me] = akv[0, me]
    for half in (0, 1):
        fq[pl.ds(half * HALF, HALF)] = (rsq.total(half) * SCALE).astype(jnp.bfloat16)
        give(lambda s: fq.at[s], out_q, fq_i, half)
    out_q[me] = fq[me]

    row_wait_send(pq, qd, xq)
    row_wait_send(pst, st, xst)
    row_wait_send(pkv, kv, xkv)
    for make, *where in sent:
        make(*where).wait_send()
    for src, dst, base in ((akv.at[0], out_kv, fkv_i), (fq, out_q, fq_i)):
        for s in range(ROW):
            @pl.when(me != s)
            def _():
                copy = remote(src.at[s], dst.at[s], base + s, base + s, row_dev(s))
                copy.wait_send()
                copy.wait_recv()


def call(queries, attn_out, grad_out, log_sum_exp, key_cache, value_cache):
    f32, bf16 = jnp.float32, jnp.bfloat16
    vmem = pltpu.VMEM
    tok = (2, TOK // 2, ROW * GRP, DIM)
    key = (KEYS, ROW, DIM)
    scratch = [
        vmem(tok, bf16), vmem(tok, bf16), vmem(tok, bf16), vmem(tok[:3], f32), vmem(key, bf16), vmem(key, bf16),
        vmem((TOK, ROW * GRP, DIM), f32), vmem(key, f32), vmem((DIM, DIM), f32), vmem((DIM, DIM), f32),
        vmem((ROW, 2 * GRP, TOK, DIM), bf16), vmem((ROW, 2, DIM), f32), vmem((ROW, 2, KEYS, DIM), bf16),
        vmem((RING, ROW, 2 * GRP, TOK, DIM), bf16), vmem((RING, ROW, 2, DIM), f32), vmem((RING, ROW, 2, KEYS, DIM), bf16),
        vmem((RING, 8, QROWS), f32), vmem((1, QROWS), jnp.int32),
        vmem((RING, ROW, 2, KEYS, DIM), f32), vmem((RING, DIM, QROWS), f32), vmem((RING, ROW, PACK, DIM), f32),
        vmem((2, HALF, 2, KEYS, DIM), f32), vmem((2, ROW, 2, KEYS, DIM), f32),
        vmem((2, HALF, PACK, DIM), f32), vmem((2, ROW, PACK, DIM), f32),
        vmem((ROW, PACK, DIM), bf16),
        pltpu.SemaphoreType.DMA((6,)), pltpu.SemaphoreType.DMA((NSEM,)), pltpu.SemaphoreType.DMA((NSEM,)),
    ]
    return pl.pallas_call(
        kernel,
        out_shape=(jax.ShapeDtypeStruct((ROW, PACK, DIM), bf16),
                   jax.ShapeDtypeStruct((ROW, 2, KEYS, DIM), f32)),
        in_specs=[pl.BlockSpec(memory_space=pl.ANY)] * 6,
        out_specs=[pl.BlockSpec(memory_space=pltpu.VMEM)] * 2,
        scratch_shapes=scratch,
        compiler_params=pltpu.CompilerParams(collective_id=0, has_side_effects=True),
        name='attn_bwd_3d',
    )(queries, attn_out, grad_out, log_sum_exp, key_cache, value_cache)


def solution(mesh):
    row_spec = P(None, CP_AXES, 'heads', None)
    stat_spec = P(None, CP_AXES, 'heads')
    key_spec = P(CP_AXES, 'heads', None)

    def local_grads(queries, attn_out, grad_out, log_sum_exp, key_cache, value_cache):
        out_q, out_kv = call(queries, attn_out, grad_out, log_sum_exp, key_cache, value_cache)
        grad_query = out_q.reshape(ROW, GRP, 2, TOK // 2, DIM).transpose(2, 3, 0, 1, 4).reshape(queries.shape)
        grad_key = out_kv[:, 0].transpose(1, 0, 2)
        grad_value = out_kv[:, 1].transpose(1, 0, 2)
        return grad_query, grad_key, grad_value

    return jax.shard_map(local_grads, mesh=mesh, in_specs=(row_spec, row_spec, row_spec, stat_spec, key_spec, key_spec),
                         out_specs=(row_spec, key_spec, key_spec), check_vma=False)
```

time: 756 us -> 48.8 us (0.06)
  waiting for transfers between devices: 554 us -> 0 us
  blocking collectives: 77.5 us -> 0 us
  local copies, waits for them, and re-layouts: 64.5 us -> 4.02 us
  Pallas kernels: 0 us -> 44 us
  matrix products: 33.1 us -> 0 us
  between operations: 14.9 us -> 0.64 us
    reduce_scatter x2 -> x0, waiting for transfers between devices: 399 us -> none  [local_grads(): lax.psum_scatter(dq_part, CP_AXES, scatter_dimension=0, tiled=True)]
    all_gather x4 -> x0, waiting for transfers between devices: 153 us -> none  [the longest x2 125 us: local_grads(): g_all = lax.all_gather(grad_out[slice_idx], CP_AXES, axis=0, tiled=True)]
    all_gather x2 -> x0, blocking collectives: 77.5 us -> none  [local_grads(): stat_all = lax.all_gather(row_stats[slice_idx], CP_AXES, axis=0, tiled=True)]
    pallas_call x0 -> x1, Pallas kernels: none -> 44 us  [call(): pl.pallas_call(kernel, out_shape=(jax.ShapeDtypeStruct((ROW, PACK, DIM),...]
    dot_general x10 -> x0, matrix products: 33.1 us -> none  [the longest x2 12 us: block_step(): jnp.einsum('hrgk,khd->rhgd', grad_scores, key_part, preferred_element_typ...]
    reshape x2 -> x0, local copies, waits for them, and re-layouts: 32.8 us -> none  [local_grads(): dq_part = dq_blocks.reshape(slice_len, q_heads, head_dim)]
    all_gather x6 -> x0, local copies, waits for them, and re-layouts: 24 us -> none  [the longest x2 13.5 us: local_grads(): q_all = lax.all_gather(queries[slice_idx], CP_AXES, axis=0, tiled=True)]
  transfers between devices with their start and end apart: 6 -> 0, of which waited for: 5 -> 0; matrix products, arithmetic and copies ran while one was open for 13% -> 0% of each run, Pallas kernels for 0% -> 0%
where the time goes in v1:
time: 48.8 us; the launch traced here: 48.6 us
  Pallas kernels  44 us (90%)
  local copies, waits for them, and re-layouts  4.02 us (8%)
  between operations  0.64 us (1%)
    pallas_call x1, Pallas kernels, call(): pl.pallas_call(kernel, out_shape=(jax.ShapeDtypeStruct((ROW, PACK, DIM),...  44 us
    unnamed x3, local copies, waits for them, and re-layouts  3.03 us
    transpose x1, local copies, waits for them, and re-layouts, local_grads(): grad_value = out_kv[:, 1].transpose(1, 0, 2)  0.99 us

profile of v1, /device:TPU:1, one launch (start us, length us, event | category | flops | bytes accessed | tf_op | source)
XLA Modules:
  0.0 48.6 jit_solution(18041205053346528659)
XLA Ops:
  0.6 44.0 %attn_bwd_3d.1 = (bf16[8,48,128]{2,1,0:T(8,128)(2,1)}, f32[8,2,32,128]{3,2,1,0:T(8,128)}) custom-call(bf16[2,8,24,128]{3,2,1,0:T(8,128)(2,1)} %q_in.1, bf16[2,8,24,128]{3,2,1,0:T(8,128)(2,1)} %o_in.1, bf16[2,8,24,128]{3,2,1,0:T(8,128)(2,1)} %g_in.1, f32[2,8,24]{2,1,0:T(8,128)} %l_in.1, bf16[32,8,128]{2,1,0:T(8,128)(2,1)} %k_in.1, bf16[32,8,128]{2,1,0:T(8,128)(2,1)} %v_in.1), custom_call_target="tpu_custom_call" | custom-call | tf_op jit(solution)/shard_map/attn_bwd_3d/pallas_call | solution.py:387
  44.6 1.6 %copy.13 = bf16[2,8,24,128]{3,2,1,0:T(8,128)(2,1)} copy(bf16[2,8,24,128]{3,1,0,2:T(8,128)(2,1)} %bitcast.13) | data formatting | bytes 196608
  46.2 1.0 %slice_bitcast_fusion = (f32[32,8,128]{2,0,1:T(8,128)S(1)}, f32[32,8,128]{2,0,1:T(8,128)S(1)}) fusion(f32[8,2,32,128]{3,2,1,0:T(8,128)} %get-tuple-element.6), kind=kLoop, calls=%fused_computation | loop fusion | bytes 524288 | tf_op jit(solution)/shard_map/transpose | solution.py:408
  47.2 0.7 %copy.15 = f32[32,8,128]{2,1,0:T(8,128)} copy(f32[32,8,128]{2,0,1:T(8,128)S(1)} %get-tuple-element.13) | data formatting | bytes 262144
  47.9 0.7 %copy.14 = f32[32,8,128]{2,1,0:T(8,128)} copy(f32[32,8,128]{2,0,1:T(8,128)S(1)} %get-tuple-element.14) | data formatting | bytes 262144

commit v2 on v1

v2 whole, which is shorter than its diff:
```python
import jax
import jax.numpy as jnp
from jax import lax
from jax.experimental import pallas as pl
from jax.experimental.pallas import tpu as pltpu
from jax.sharding import PartitionSpec as P

CP_AXES = ('cpo', 'cp')
MESH = pl.DeviceIdType.MESH
LOG2E = 1.4426950408889634

ROW = 8
RING = 4
GRP = 3
TOK = 16
KEYS = 32
DIM = 128
HALF = ROW // 2
QROWS = ROW * GRP * TOK
KROWS = ROW * KEYS
PACK = GRP * TOK
SCALE = DIM ** -0.5
NSEM = 96
OWN, F, G, X = range(4)

NT = (((1,), (1,)), ((), ()))
NN = (((1,), (0,)), ((), ()))
TN = (((0,), (0,)), ((), ()))


def dot(a, b, dims):
    return lax.dot_general(a, b, dims, preferred_element_type=jnp.float32)


def kernel(q_in, o_in, g_in, l_in, k_in, v_in, out_q, out_kv,
           q_vm, o_vm, g_vm, l_vm, k_vm, v_vm, xs, xk, ts, tt,
           pq, pst, pkv, qd, st, kv, ld, rowc, akv, aqt, oq,
           ra_kv, rb_kv, ra_q, rb_q, fq, in_sem, ssem, rsem):
    me = lax.axis_index('cp')
    cpo = lax.axis_index('cpo')
    z, y = cpo // RING, cpo % RING

    def row_dev(j):
        return (0, cpo, j)

    def ring_devs(axis):
        if axis == 'y':
            return [(0, z * RING + (y + d) % RING, me) for d in (1, 3)]
        return [(0, ((z + d) % RING) * RING + y, me) for d in (1, 3)]

    ydev, zdev = ring_devs('y'), ring_devs('z')

    barrier = pltpu.get_barrier_semaphore()
    for j in range(1, ROW):
        pl.semaphore_signal(barrier, inc=1, device_id=row_dev((me + j) % ROW), device_id_type=MESH)
    for dev in ydev + zdev:
        pl.semaphore_signal(barrier, inc=1, device_id=dev, device_id_type=MESH)

    loads = [pltpu.make_async_copy(src, dst, in_sem.at[i]) for i, (src, dst) in enumerate(
        ((g_in, g_vm), (o_in, o_vm), (q_in, q_vm), (l_in, l_vm), (k_in, k_vm), (v_in, v_vm)))]
    for ld_copy in loads:
        ld_copy.start()

    counter = [0]

    def take(n):
        first = counter[0]
        counter[0] += n
        assert counter[0] <= NSEM
        return first

    def remote(src, dst, send_i, recv_i, dev):
        return pltpu.make_async_remote_copy(
            src_ref=src, dst_ref=dst, send_sem=ssem.at[send_i], recv_sem=rsem.at[recv_i],
            device_id=dev, device_id_type=MESH)

    sent = []

    loads[0].wait()
    loads[1].wait()
    gf = g_vm[...].reshape(TOK, ROW * GRP, DIM).astype(jnp.float32)
    xs[...] = gf
    of = o_vm[...].reshape(TOK, ROW * GRP, DIM).astype(jnp.float32)
    delta = jnp.sum(gf * of, axis=-1)
    ts[...] = jnp.zeros_like(ts)
    loads[3].wait()
    ts[pl.ds(0, TOK), pl.ds(0, ROW * GRP)] = l_vm[...].reshape(TOK, ROW * GRP)
    ts[pl.ds(TOK, TOK), pl.ds(0, ROW * GRP)] = delta
    for h in range(ROW):
        for g in range(GRP):
            pq[h, GRP + g] = xs[:, h * GRP + g, :].astype(jnp.bfloat16)
    loads[2].wait()
    xs[...] = q_vm[...].reshape(TOK, ROW * GRP, DIM).astype(jnp.float32)
    for h in range(ROW):
        for g in range(GRP):
            pq[h, g] = xs[:, h * GRP + g, :].astype(jnp.bfloat16)
    tt[...] = ts[...].T
    lane = lax.broadcasted_iota(jnp.int32, (ROW, DIM), 1)
    for which in range(2):
        packed = jnp.zeros((ROW, DIM), jnp.float32)
        for g in range(GRP):
            part = tt[pl.ds(g, ROW, stride=GRP), :]
            shift = (g * TOK - which * TOK) % DIM
            if shift:
                part = pltpu.roll(part, shift, 1)
            packed = jnp.where((lane >= g * TOK) & (lane < (g + 1) * TOK), part, packed)
        pst[:, which, :] = pltpu.roll(packed, (PACK * me) % DIM, 1)

    with jax.named_scope('barrier'):
        pl.semaphore_wait(barrier, ROW - 1 + 4)

    def row_send(src, dst, base):
        for j in (4, 5, 2, 3, 6, 7, 1):
            d = (me + j) % ROW
            remote(src.at[d], dst.at[0, me], base + d, base + me, row_dev(d)).start()

    def row_wait(buf, base, s):
        @pl.when(me != s)
        def _():
            remote(buf.at[0, s], buf.at[0, s], base + s, base + s, row_dev(s)).wait_recv()

    def row_wait_send(src, dst, base):
        for j in range(1, ROW):
            d = (me + j) % ROW
            remote(src.at[d], dst.at[0, me], base + d, base + me, row_dev(d)).wait_send()

    xq, xst, xkv = take(ROW), take(ROW), take(ROW)
    row_send(pq, qd, xq)
    row_send(pst, st, xst)
    qd[0, me] = pq[me]
    st[0, me] = pst[me]

    loads[4].wait()
    xk[...] = k_vm[...].astype(jnp.float32)
    for h in range(ROW):
        pkv[h, 0] = xk[:, h, :].astype(jnp.bfloat16)
    loads[5].wait()
    xk[...] = v_vm[...].astype(jnp.float32)
    for h in range(ROW):
        pkv[h, 1] = xk[:, h, :].astype(jnp.bfloat16)
    row_send(pkv, kv, xkv)
    kv[0, me] = pkv[me]

    akv[...] = jnp.zeros_like(akv)
    aqt[...] = jnp.zeros_like(aqt)

    def offset(group, half):
        near = (1, 3) if half else (3, 1)
        return jnp.where(group == F, near[0], jnp.where(group == G, near[1], jnp.where(group == X, 2, 0)))

    def part(ref, half):
        return ref.at[pl.ds(half * HALF, HALF)]

    r_id = lax.broadcasted_iota(jnp.int32, (1, QROWS), 1)
    token = ((r_id >> 3) & 1) * 1024 + ((r_id * 1366) >> 16) * 8 + (r_id & 7) + (2048 + z * 256)
    for group in range(RING):
        plane = jnp.where(r_id < QROWS // 2, (y + offset(group, 0)) % RING, (y + offset(group, 1)) % RING)
        rowc[group] = token + plane * 64

    class Gather:
        def __init__(self, buf, devs):
            self.buf, self.devs = buf, devs
            self.near = take(4)
            self.far = take(2)

        def near_copy(self, group, half):
            i = self.near + (group - F) * 2 + half
            dev = self.devs[half if group == F else 1 - half]
            return remote(part(self.buf.at[OWN], half), part(self.buf.at[group], half), i, i, dev)

        def far_copy(self, half):
            i = self.far + half
            return remote(part(self.buf.at[F], half), part(self.buf.at[X], half), i, i, self.devs[half])

        def send(self, group):
            for half in (0, 1):
                self.near_copy(group, half).start()
                sent.append((self.near_copy, group, half))

        def wait(self, group):
            for half in (0, 1):
                self.near_copy(group, half).wait_recv()

        def forward(self, half):
            self.near_copy(F, half).wait_recv()
            self.far_copy(half).start()
            sent.append((self.far_copy, half))

        def wait_far(self):
            for half in (0, 1):
                self.far_copy(half).wait_recv()

    agq, agst, agkv = Gather(qd, ydev), Gather(st, ydev), Gather(kv, zdev)
    with jax.named_scope('wait_row_q'):
        for s in range(ROW):
            row_wait(qd, xq, s)
            row_wait(st, xst, s)
    agq.send(F)
    agst.send(F)
    agq.send(G)
    agst.send(G)
    with jax.named_scope('wait_row_kv'):
        for s in range(ROW):
            row_wait(kv, xkv, s)
    agkv.send(F)
    agkv.send(G)

    src_id = lax.broadcasted_iota(jnp.int32, (ROW, DIM), 0)

    def assemble(group):
        for which in range(2):
            rows = st[group, :, which, :]
            for k in range(QROWS // DIM):
                mine = (((lane + k * DIM) * 1366) >> 16) == src_id
                line = jnp.sum(jnp.where(mine, rows, 0.0), axis=0, keepdims=True)
                ld[group, pl.ds(which, 1), pl.ds(k * DIM, DIM)] = line * LOG2E if which == 0 else line

    class Scatter:
        def __init__(self, acc, ra, rb, devs):
            self.acc, self.ra, self.rb, self.devs = acc, ra, rb, devs
            self.first = take(2)
            self.second = take(4)

        def far_copy(self, half):
            i = self.first + half
            return remote(part(self.acc(X), half), self.ra.at[half], i, i, self.devs[half])

        def early_copy(self, half):
            i = self.second + half
            return remote(part(self.acc(F), half), part(self.rb.at[1 - half], half), i, i, self.devs[1 - half])

        def late_copy(self, half):
            i = self.second + 2 + half
            return remote(part(self.acc(G), half), part(self.rb.at[half], half), i, i, self.devs[half])

        def start(self, make):
            for half in (0, 1):
                make(half).start()
                sent.append((make, half))

        def send_late(self):
            for half in (0, 1):
                self.far_copy(half).wait_recv()
                mine = part(self.acc(G), half)
                mine[...] = mine[...] + self.ra[half]
                self.late_copy(half).start()
                sent.append((self.late_copy, half))

        def total(self, half):
            self.early_copy(half).wait_recv()
            self.late_copy(half).wait_recv()
            return part(self.acc(OWN), half)[...] + part(self.rb.at[0], half)[...] + part(self.rb.at[1], half)[...]

    rsk = Scatter(lambda group: akv.at[group, 0], ra_kv.at[0], rb_kv.at[0], zdev)
    rsv = Scatter(lambda group: akv.at[group, 1], ra_kv.at[1], rb_kv.at[1], zdev)
    rsq = Scatter(lambda group: oq.at[group], ra_q, rb_q, ydev)

    half_rows = KROWS // 2
    key_row = lax.broadcasted_iota(jnp.int32, (half_rows, QROWS), 0)

    def block(qs, ks):
        q = qd[qs, :, pl.ds(0, GRP)].reshape(QROWS, DIM)
        g = qd[qs, :, pl.ds(GRP, GRP)].reshape(QROWS, DIM)
        k = kv[ks, :, 0].reshape(KROWS, DIM)
        v = kv[ks, :, 1].reshape(KROWS, DIM)
        lse = ld[qs, pl.ds(0, 1), :]
        dlt = ld[qs, pl.ds(1, 1), :]
        s_t = dot(k, q, NT)
        halves = []
        for half in (0, 1):
            first = ((z + offset(ks, half)) % RING) * 1024 + y * 256 + half * half_rows
            rows = s_t[half * half_rows:(half + 1) * half_rows]
            halves.append(jnp.where(key_row <= rowc[qs] - first, jnp.exp2(rows * (SCALE * LOG2E) - lse), 0.0))
        p_t = jnp.concatenate(halves, axis=0)
        dp_t = dot(v, g, NT)
        ds_t = (p_t * (dp_t - dlt)).astype(jnp.bfloat16)
        akv[ks, 1] = akv[ks, 1] + dot(p_t.astype(jnp.bfloat16), g, NN).reshape(ROW, KEYS, DIM)
        akv[ks, 0] = akv[ks, 0] + dot(ds_t, q, NN).reshape(ROW, KEYS, DIM)
        aqt[qs] = aqt[qs] + dot(k, ds_t, TN)

    def finish_q(group):
        oq[group] = aqt[group].T.reshape(ROW, PACK, DIM)

    def before_0():
        for half in (0, 1):
            agq.forward(half)
            agst.forward(half)
        for half in (0, 1):
            agkv.forward(half)
        assemble(F)

    def before_1():
        agkv.wait(G)

    def before_2():
        agq.wait(G)
        agst.wait(G)
        assemble(G)

    def before_4():
        agkv.wait_far()

    def before_5():
        agq.wait_far()
        agst.wait_far()
        assemble(X)

    def after_4():
        finish_q(OWN)
        finish_q(G)

    def after_5():
        rsv.start(rsv.far_copy)
        rsk.start(rsk.far_copy)
        finish_q(F)
        rsq.start(rsq.early_copy)

    def after_6():
        rsv.start(rsv.early_copy)

    before = {0: before_0, 1: before_1, 2: before_2, 4: before_4, 5: before_5}
    after = {4: after_4, 5: after_5, 6: after_6}
    pairs = (((OWN, F), (F, F)), ((F, OWN), (OWN, G)), ((F, G), (G, OWN)), ((G, F), (G, G)),
             ((G, X), (OWN, X)), ((F, X), (X, X)), ((X, F), (X, G)))

    def pick(i, values):
        out = values[-1]
        for n in range(len(values) - 1):
            out = jnp.where(i == n, values[n], out)
        return out

    def step(i, carry):
        for n, act in before.items():
            @pl.when(i == n)
            def _(n=n, act=act):
                with jax.named_scope(f'before_{n}'):
                    act()
        with jax.named_scope('pair'):
            for j in (0, 1):
                block(pick(i, [pair[j][0] for pair in pairs]), pick(i, [pair[j][1] for pair in pairs]))
        for n, act in after.items():
            @pl.when(i == n)
            def _(n=n, act=act):
                with jax.named_scope(f'after_{n}'):
                    act()
        return carry

    assemble(OWN)
    with jax.named_scope('first'):
        block(OWN, OWN)
    lax.fori_loop(0, len(pairs), step, 0)
    with jax.named_scope('last'):
        block(X, OWN)
    finish_q(X)
    rsq.start(rsq.far_copy)

    with jax.named_scope('late_v'):
        rsv.send_late()
    rsk.start(rsk.early_copy)
    with jax.named_scope('late_k'):
        rsk.send_late()
    with jax.named_scope('late_q'):
        rsq.send_late()

    fk_i, fv_i, fq_i = take(ROW), take(ROW), take(ROW)

    def give(src, dst, base, half):
        for s in range(half * HALF, (half + 1) * HALF):
            @pl.when(me != s)
            def _():
                remote(src.at[s], dst.at[me], base + s, base + me, row_dev(s)).start()

    own_k, own_v = akv.at[OWN, 0], akv.at[OWN, 1]
    for half in (0, 1):
        with jax.named_scope('total_v'):
            part(own_v, half)[...] = rsv.total(half)
        give(own_v, out_kv.at[1], fv_i, half)
    out_kv[1, me] = akv[OWN, 1, me]
    for half in (0, 1):
        with jax.named_scope('total_q'):
            fq[pl.ds(half * HALF, HALF)] = (rsq.total(half) * SCALE).astype(jnp.bfloat16)
        give(fq, out_q, fq_i, half)
    out_q[me] = fq[me]
    for half in (0, 1):
        with jax.named_scope('total_k'):
            part(own_k, half)[...] = rsk.total(half) * SCALE
        give(own_k, out_kv.at[0], fk_i, half)
    out_kv[0, me] = akv[OWN, 0, me]

    with jax.named_scope('drain'):
        row_wait_send(pq, qd, xq)
        row_wait_send(pst, st, xst)
        row_wait_send(pkv, kv, xkv)
        for make, *where in sent:
            make(*where).wait_send()
    for name, src, dst, base in (('v', own_v, out_kv.at[1], fv_i), ('q', fq, out_q, fq_i), ('k', own_k, out_kv.at[0], fk_i)):
        with jax.named_scope('final_' + name):
            for s in range(ROW):
                @pl.when(me != s)
                def _():
                    copy = remote(src.at[s], dst.at[s], base + s, base + s, row_dev(s))
                    copy.wait_send()
                    copy.wait_recv()


def relayout(q_ref, kv_ref, dq_ref, dk_ref, dv_ref, rows):
    for h in range(ROW):
        dk_ref[:, h, :] = kv_ref[0, h]
        dv_ref[:, h, :] = kv_ref[1, h]
        for g in range(GRP):
            rows[:, h * GRP + g, :] = q_ref[h, pl.ds(g * TOK, TOK), :].astype(jnp.float32)
    dq_ref[...] = rows[...].astype(jnp.bfloat16).reshape(dq_ref.shape)


def call(queries, attn_out, grad_out, log_sum_exp, key_cache, value_cache):
    f32, bf16 = jnp.float32, jnp.bfloat16
    vmem = pltpu.VMEM
    tok = (2, TOK // 2, ROW * GRP, DIM)
    key = (KEYS, ROW, DIM)
    scratch = [
        vmem(tok, bf16), vmem(tok, bf16), vmem(tok, bf16), vmem(tok[:3], f32), vmem(key, bf16), vmem(key, bf16),
        vmem((TOK, ROW * GRP, DIM), f32), vmem(key, f32), vmem((DIM, DIM), f32), vmem((DIM, DIM), f32),
        vmem((ROW, 2 * GRP, TOK, DIM), bf16), vmem((ROW, 2, DIM), f32), vmem((ROW, 2, KEYS, DIM), bf16),
        vmem((RING, ROW, 2 * GRP, TOK, DIM), bf16), vmem((RING, ROW, 2, DIM), f32), vmem((RING, ROW, 2, KEYS, DIM), bf16),
        vmem((RING, 8, QROWS), f32), vmem((RING, 1, QROWS), jnp.int32),
        vmem((RING, 2, ROW, KEYS, DIM), f32), vmem((RING, DIM, QROWS), f32), vmem((RING, ROW, PACK, DIM), f32),
        vmem((2, 2, HALF, KEYS, DIM), f32), vmem((2, 2, ROW, KEYS, DIM), f32),
        vmem((2, HALF, PACK, DIM), f32), vmem((2, ROW, PACK, DIM), f32),
        vmem((ROW, PACK, DIM), bf16),
        pltpu.SemaphoreType.DMA((6,)), pltpu.SemaphoreType.DMA((NSEM,)), pltpu.SemaphoreType.DMA((NSEM,)),
    ]
    out_q, out_kv = pl.pallas_call(
        kernel,
        out_shape=(jax.ShapeDtypeStruct((ROW, PACK, DIM), bf16),
                   jax.ShapeDtypeStruct((2, ROW, KEYS, DIM), f32)),
        in_specs=[pl.BlockSpec(memory_space=pl.ANY)] * 6,
        out_specs=[pl.BlockSpec(memory_space=pltpu.VMEM)] * 2,
        scratch_shapes=scratch,
        compiler_params=pltpu.CompilerParams(collective_id=0, has_side_effects=True),
        name='attn_bwd_3d',
    )(queries, attn_out, grad_out, log_sum_exp, key_cache, value_cache)
    return pl.pallas_call(
        relayout,
        out_shape=(jax.ShapeDtypeStruct(tok, bf16), jax.ShapeDtypeStruct(key, f32), jax.ShapeDtypeStruct(key, f32)),
        in_specs=[pl.BlockSpec(memory_space=pltpu.VMEM)] * 2,
        out_specs=[pl.BlockSpec(memory_space=pltpu.VMEM)] * 3,
        scratch_shapes=[vmem((TOK, ROW * GRP, DIM), f32)],
        name='relayout',
    )(out_q, out_kv)


def solution(mesh):
    row_spec = P(None, CP_AXES, 'heads', None)
    stat_spec = P(None, CP_AXES, 'heads')
    key_spec = P(CP_AXES, 'heads', None)
    return jax.shard_map(call, mesh=mesh, in_specs=(row_spec, row_spec, row_spec, stat_spec, key_spec, key_spec),
                         out_specs=(row_spec, key_spec, key_spec), check_vma=False)
```

time: 48.8 us -> 43.8 us (0.90)
  local copies, waits for them, and re-layouts: 4.02 us -> 0 us
  Pallas kernels: 44 us -> 43 us
    unnamed x3 -> x0, local copies, waits for them, and re-layouts: 3.03 us -> none
    pallas_call x1, Pallas kernels: 44 us -> 41.1 us  [call(): pl.pallas_call(kernel, out_shape=(jax.ShapeDtypeStruct((ROW, PACK, DIM),...]
    pallas_call x0 -> x1, Pallas kernels: none -> 1.93 us  [call(): pl.pallas_call(relayout, out_shape=(jax.ShapeDtypeStruct(tok, bf16), jax....]
    transpose x1 -> x0, local copies, waits for them, and re-layouts: 0.99 us -> none  [local_grads(): grad_value = out_kv[:, 1].transpose(1, 0, 2)]
where the time goes in v2:
time: 43.8 us; the launch traced here: 43.6 us
  Pallas kernels  43 us (98%)
  between operations  0.64 us (1%)
    pallas_call x1, Pallas kernels, call(): pl.pallas_call(kernel, out_shape=(jax.ShapeDtypeStruct((ROW, PACK, DIM),...  41.1 us
    pallas_call x1, Pallas kernels, call(): pl.pallas_call(relayout, out_shape=(jax.ShapeDtypeStruct(tok, bf16), jax....  1.93 us

profile of v2, /device:TPU:1, one launch (start us, length us, event | category | flops | bytes accessed | tf_op | source)
XLA Modules:
  0.0 43.6 jit_solution(10140136895924134876)
XLA Ops:
  0.6 41.1 %attn_bwd_3d.1 = (bf16[8,48,128]{2,1,0:T(8,128)(2,1)}, f32[2,8,32,128]{3,2,1,0:T(8,128)}) custom-call(bf16[2,8,24,128]{3,2,1,0:T(8,128)(2,1)} %q_in.1, bf16[2,8,24,128]{3,2,1,0:T(8,128)(2,1)} %o_in.1, bf16[2,8,24,128]{3,2,1,0:T(8,128)(2,1)} %g_in.1, f32[2,8,24]{2,1,0:T(8,128)} %l_in.1, bf16[32,8,128]{2,1,0:T(8,128)(2,1)} %k_in.1, bf16[32,8,128]{2,1,0:T(8,128)(2,1)} %v_in.1), custom_call_target="tpu_custom_call" | custom-call | tf_op jit(solution)/shard_map/attn_bwd_3d/pallas_call | solution.py:432
  41.7 1.9 %relayout.1 = (bf16[2,8,24,128]{3,2,1,0:T(8,128)(2,1)}, f32[32,8,128]{2,1,0:T(8,128)}, f32[32,8,128]{2,1,0:T(8,128)}) custom-call(bf16[8,48,128]{2,1,0:T(8,128)(2,1)} %get-tuple-element.5.q_ref, f32[2,8,32,128]{3,2,1,0:T(8,128)} %get-tuple-element.6.kv_ref), custom_call_target="tpu_custom_call" | custom-call | tf_op jit(solution)/shard_map/relayout/pallas_call | solution.py:442

commit v3 on v2

--- a/solution.py
+++ b/solution.py
@@ -20,7 +20,8 @@
 KROWS = ROW * KEYS
 PACK = GRP * TOK
 SCALE = DIM ** -0.5
-NSEM = 96
+NSEM = 30
+NSEND = 12
 OWN, F, G, X = range(4)
 
 NT = (((1,), (1,)), ((), ()))
@@ -61,7 +62,7 @@
     for ld_copy in loads:
         ld_copy.start()
 
-    counter = [0]
+    counter = [0, 0]
 
     def take(n):
         first = counter[0]
@@ -69,10 +70,18 @@
         assert counter[0] <= NSEM
         return first
 
+    def take_send():
+        counter[1] += 1
+        assert counter[1] <= NSEND
+        return counter[1] - 1
+
     def remote(src, dst, send_i, recv_i, dev):
         return pltpu.make_async_remote_copy(
             src_ref=src, dst_ref=dst, send_sem=ssem.at[send_i], recv_sem=rsem.at[recv_i],
             device_id=dev, device_id_type=MESH)
+
+    def arrived(ref, recv_i):
+        remote(ref, ref, 0, recv_i, row_dev(me)).wait_recv()
 
     sent = []
 
@@ -109,26 +118,18 @@
     with jax.named_scope('barrier'):
         pl.semaphore_wait(barrier, ROW - 1 + 4)
 
-    def row_send(src, dst, base):
+    def row_send(src, dst):
+        send_i, recv_i = take_send(), take(1)
         for j in (4, 5, 2, 3, 6, 7, 1):
             d = (me + j) % ROW
-            remote(src.at[d], dst.at[0, me], base + d, base + me, row_dev(d)).start()
-
-    def row_wait(buf, base, s):
-        @pl.when(me != s)
-        def _():
-            remote(buf.at[0, s], buf.at[0, s], base + s, base + s, row_dev(s)).wait_recv()
-
-    def row_wait_send(src, dst, base):
-        for j in range(1, ROW):
-            d = (me + j) % ROW
-            remote(src.at[d], dst.at[0, me], base + d, base + me, row_dev(d)).wait_send()
-
-    xq, xst, xkv = take(ROW), take(ROW), take(ROW)
-    row_send(pq, qd, xq)
-    row_send(pst, st, xst)
-    qd[0, me] = pq[me]
-    st[0, me] = pst[me]
+            remote(src.at[d], dst.at[me], send_i, recv_i, row_dev(d)).start()
+        sent.append((send_i, src.at[pl.ds(0, ROW - 1)]))
+        return lambda: arrived(dst.at[pl.ds(0, ROW - 1)], recv_i)
+
+    row_q = row_send(pq, qd.at[OWN])
+    row_st = row_send(pst, st.at[OWN])
+    qd[OWN, me] = pq[me]
+    st[OWN, me] = pst[me]
 
     loads[4].wait()
     xk[...] = k_vm[...].astype(jnp.float32)
@@ -138,8 +139,8 @@
     xk[...] = v_vm[...].astype(jnp.float32)
     for h in range(ROW):
         pkv[h, 1] = xk[:, h, :].astype(jnp.bfloat16)
-    row_send(pkv, kv, xkv)
-    kv[0, me] = pkv[me]
+    row_kv = row_send(pkv, kv.at[OWN])
+    kv[OWN, me] = pkv[me]
 
     akv[...] = jnp.zeros_like(akv)
     aqt[...] = jnp.zeros_like(aqt)
@@ -160,48 +161,36 @@
     class Gather:
         def __init__(self, buf, devs):
             self.buf, self.devs = buf, devs
-            self.near = take(4)
-            self.far = take(2)
-
-        def near_copy(self, group, half):
-            i = self.near + (group - F) * 2 + half
-            dev = self.devs[half if group == F else 1 - half]
-            return remote(part(self.buf.at[OWN], half), part(self.buf.at[group], half), i, i, dev)
-
-        def far_copy(self, half):
-            i = self.far + half
-            return remote(part(self.buf.at[F], half), part(self.buf.at[X], half), i, i, self.devs[half])
+            self.send_i, self.first, self.second, self.far = take_send(), take(2), take(1), take(1)
+            sent.append((self.send_i, buf.at[pl.ds(0, RING - 1)]))
 
         def send(self, group):
             for half in (0, 1):
-                self.near_copy(group, half).start()
-                sent.append((self.near_copy, group, half))
-
-        def wait(self, group):
-            for half in (0, 1):
-                self.near_copy(group, half).wait_recv()
+                dev = self.devs[half if group == F else 1 - half]
+                recv_i = self.first + half if group == F else self.second
+                remote(part(self.buf.at[OWN], half), part(self.buf.at[group], half), self.send_i, recv_i, dev).start()
 
         def forward(self, half):
-            self.near_copy(F, half).wait_recv()
-            self.far_copy(half).start()
-            sent.append((self.far_copy, half))
+            mine = part(self.buf.at[F], half)
+            arrived(mine, self.first + half)
+            remote(mine, part(self.buf.at[X], half), self.send_i, self.far, self.devs[half]).start()
+
+        def wait_second(self):
+            arrived(self.buf.at[G], self.second)
 
         def wait_far(self):
-            for half in (0, 1):
-                self.far_copy(half).wait_recv()
+            arrived(self.buf.at[X], self.far)
 
     agq, agst, agkv = Gather(qd, ydev), Gather(st, ydev), Gather(kv, zdev)
     with jax.named_scope('wait_row_q'):
-        for s in range(ROW):
-            row_wait(qd, xq, s)
-            row_wait(st, xst, s)
+        row_q()
+        row_st()
     agq.send(F)
     agst.send(F)
     agq.send(G)
     agst.send(G)
     with jax.named_scope('wait_row_kv'):
-        for s in range(ROW):
-            row_wait(kv, xkv, s)
+        row_kv()
     agkv.send(F)
     agkv.send(G)
 
@@ -218,42 +207,34 @@
     class Scatter:
         def __init__(self, acc, ra, rb, devs):
             self.acc, self.ra, self.rb, self.devs = acc, ra, rb, devs
-            self.first = take(2)
-            self.second = take(4)
-
-        def far_copy(self, half):
-            i = self.first + half
-            return remote(part(self.acc(X), half), self.ra.at[half], i, i, self.devs[half])
-
-        def early_copy(self, half):
-            i = self.second + half
-            return remote(part(self.acc(F), half), part(self.rb.at[1 - half], half), i, i, self.devs[1 - half])
-
-        def late_copy(self, half):
-            i = self.second + 2 + half
-            return remote(part(self.acc(G), half), part(self.rb.at[half], half), i, i, self.devs[half])
-
-        def start(self, make):
+            self.send_i, self.first, self.near = take_send(), take(2), take(2)
+            sent.append((self.send_i, acc.at[pl.ds(0, RING - 1)]))
+
+        def send(self, group, half, dst, recv_i, dev):
+            remote(part(self.acc.at[group], half), dst, self.send_i, recv_i, dev).start()
+
+        def send_far(self):
             for half in (0, 1):
-                make(half).start()
-                sent.append((make, half))
+                self.send(X, half, self.ra.at[half], self.first + half, self.devs[half])
+
+        def send_early(self):
+            for half in (0, 1):
+                self.send(F, half, part(self.rb.at[1 - half], half), self.near + half, self.devs[1 - half])
 
         def send_late(self):
             for half in (0, 1):
-                self.far_copy(half).wait_recv()
-                mine = part(self.acc(G), half)
+                arrived(self.ra.at[half], self.first + half)
+                mine = part(self.acc.at[G], half)
                 mine[...] = mine[...] + self.ra[half]
-                self.late_copy(half).start()
-                sent.append((self.late_copy, half))
+                self.send(G, half, part(self.rb.at[half], half), self.near + half, self.devs[half])
 
         def total(self, half):
-            self.early_copy(half).wait_recv()
-            self.late_copy(half).wait_recv()
-            return part(self.acc(OWN), half)[...] + part(self.rb.at[0], half)[...] + part(self.rb.at[1], half)[...]
-
-    rsk = Scatter(lambda group: akv.at[group, 0], ra_kv.at[0], rb_kv.at[0], zdev)
-    rsv = Scatter(lambda group: akv.at[group, 1], ra_kv.at[1], rb_kv.at[1], zdev)
-    rsq = Scatter(lambda group: oq.at[group], ra_q, rb_q, ydev)
+            arrived(self.rb.at[0], self.near + half)
+            return part(self.acc.at[OWN], half)[...] + part(self.rb.at[0], half)[...] + part(self.rb.at[1], half)[...]
+
+    rsk = Scatter(akv.at[0], ra_kv.at[0], rb_kv.at[0], zdev)
+    rsv = Scatter(akv.at[1], ra_kv.at[1], rb_kv.at[1], zdev)
+    rsq = Scatter(oq, ra_q, rb_q, ydev)
 
     half_rows = KROWS // 2
     key_row = lax.broadcasted_iota(jnp.int32, (half_rows, QROWS), 0)
@@ -274,8 +255,8 @@
         p_t = jnp.concatenate(halves, axis=0)
         dp_t = dot(v, g, NT)
         ds_t = (p_t * (dp_t - dlt)).astype(jnp.bfloat16)
-        akv[ks, 1] = akv[ks, 1] + dot(p_t.astype(jnp.bfloat16), g, NN).reshape(ROW, KEYS, DIM)
-        akv[ks, 0] = akv[ks, 0] + dot(ds_t, q, NN).reshape(ROW, KEYS, DIM)
+        akv[1, ks] = akv[1, ks] + dot(p_t.astype(jnp.bfloat16), g, NN).reshape(ROW, KEYS, DIM)
+        akv[0, ks] = akv[0, ks] + dot(ds_t, q, NN).reshape(ROW, KEYS, DIM)
         aqt[qs] = aqt[qs] + dot(k, ds_t, TN)
 
     def finish_q(group):
@@ -290,11 +271,11 @@
         assemble(F)
 
     def before_1():
-        agkv.wait(G)
+        agkv.wait_second()
 
     def before_2():
-        agq.wait(G)
-        agst.wait(G)
+        agq.wait_second()
+        agst.wait_second()
         assemble(G)
 
     def before_4():
@@ -310,13 +291,13 @@
         finish_q(G)
 
     def after_5():
-        rsv.start(rsv.far_copy)
-        rsk.start(rsk.far_copy)
+        rsv.send_far()
+        rsk.send_far()
         finish_q(F)
-        rsq.start(rsq.early_copy)
+        rsq.send_early()
 
     def after_6():
-        rsv.start(rsv.early_copy)
+        rsv.send_early()
 
     before = {0: before_0, 1: before_1, 2: before_2, 4: before_4, 5: before_5}
     after = {4: after_4, 5: after_5, 6: after_6}
@@ -352,55 +333,58 @@
     with jax.named_scope('last'):
         block(X, OWN)
     finish_q(X)
-    rsq.start(rsq.far_copy)
+    rsq.send_far()
 
     with jax.named_scope('late_v'):
         rsv.send_late()
-    rsk.start(rsk.early_copy)
+    rsk.send_early()
     with jax.named_scope('late_k'):
         rsk.send_late()
     with jax.named_scope('late_q'):
         rsq.send_late()
 
-    fk_i, fv_i, fq_i = take(ROW), take(ROW), take(ROW)
-
-    def give(src, dst, base, half):
-        for s in range(half * HALF, (half + 1) * HALF):
-            @pl.when(me != s)
-            def _():
-                remote(src.at[s], dst.at[me], base + s, base + me, row_dev(s)).start()
-
-    own_k, own_v = akv.at[OWN, 0], akv.at[OWN, 1]
+    class Give:
+        def __init__(self, src, dst):
+            self.src, self.dst = src, dst
+            self.send_i, self.recv_i = take_send(), take(1)
+            sent.append((self.send_i, src.at[pl.ds(0, ROW - 1)]))
+
+        def send(self, half):
+            for s in range(half * HALF, (half + 1) * HALF):
+                @pl.when(me != s)
+                def _():
+                    remote(self.src.at[s], self.dst.at[me], self.send_i, self.recv_i, row_dev(s)).start()
+
+        def wait(self):
+            arrived(self.dst.at[pl.ds(0, ROW - 1)], self.recv_i)
+
+    own_k, own_v = akv.at[0, OWN], akv.at[1, OWN]
+    give_k, give_v, give_q = Give(own_k, out_kv.at[0]), Give(own_v, out_kv.at[1]), Give(fq, out_q)
     for half in (0, 1):
         with jax.named_scope('total_v'):
             part(own_v, half)[...] = rsv.total(half)
-        give(own_v, out_kv.at[1], fv_i, half)
-    out_kv[1, me] = akv[OWN, 1, me]
+        give_v.send(half)
+    out_kv[1, me] = akv[1, OWN, me]
     for half in (0, 1):
         with jax.named_scope('total_q'):
             fq[pl.ds(half * HALF, HALF)] = (rsq.total(half) * SCALE).astype(jnp.bfloat16)
-        give(fq, out_q, fq_i, half)
+        give_q.send(half)
     out_q[me] = fq[me]
     for half in (0, 1):
         with jax.named_scope('total_k'):
             part(own_k, half)[...] = rsk.total(half) * SCALE
-        give(own_k, out_kv.at[0], fk_i, half)
-    out_kv[0, me] = akv[OWN, 0, me]
+        give_k.send(half)
+    out_kv[0, me] = akv[0, OWN, me]
 
     with jax.named_scope('drain'):
-        row_wait_send(pq, qd, xq)
-        row_wait_send(pst, st, xst)
-        row_wait_send(pkv, kv, xkv)
-        for make, *where in sent:
-            make(*where).wait_send()
-    for name, src, dst, base in (('v', own_v, out_kv.at[1], fv_i), ('q', fq, out_q, fq_i), ('k', own_k, out_kv.at[0], fk_i)):
-        with jax.named_scope('final_' + name):
-            for s in range(ROW):
-                @pl.when(me != s)
-                def _():
-                    copy = remote(src.at[s], dst.at[s], base + s, base + s, row_dev(s))
-                    copy.wait_send()
-                    copy.wait_recv()
+        for send_i, ref in sent:
+            remote(ref, ref, send_i, 0, row_dev(me)).wait_send()
+    with jax.named_scope('final_v'):
+        give_v.wait()
+    with jax.named_scope('final_q'):
+        give_q.wait()
+    with jax.named_scope('final_k'):
+        give_k.wait()
 
 
 def relayout(q_ref, kv_ref, dq_ref, dk_ref, dv_ref, rows):
@@ -423,16 +407,15 @@
         vmem((ROW, 2 * GRP, TOK, DIM), bf16), vmem((ROW, 2, DIM), f32), vmem((ROW, 2, KEYS, DIM), bf16),
         vmem((RING, ROW, 2 * GRP, TOK, DIM), bf16), vmem((RING, ROW, 2, DIM), f32), vmem((RING, ROW, 2, KEYS, DIM), bf16),
         vmem((RING, 8, QROWS), f32), vmem((RING, 1, QROWS), jnp.int32),
-        vmem((RING, 2, ROW, KEYS, DIM), f32), vmem((RING, DIM, QROWS), f32), vmem((RING, ROW, PACK, DIM), f32),
+        vmem((2, RING, ROW, KEYS, DIM), f32), vmem((RING, DIM, QROWS), f32), vmem((RING, ROW, PACK, DIM), f32),
         vmem((2, 2, HALF, KEYS, DIM), f32), vmem((2, 2, ROW, KEYS, DIM), f32),
         vmem((2, HALF, PACK, DIM), f32), vmem((2, ROW, PACK, DIM), f32),
         vmem((ROW, PACK, DIM), bf16),
-        pltpu.SemaphoreType.DMA((6,)), pltpu.SemaphoreType.DMA((NSEM,)), pltpu.SemaphoreType.DMA((NSEM,)),
+        pltpu.SemaphoreType.DMA((6,)), pltpu.SemaphoreType.DMA((NSEND,)), pltpu.SemaphoreType.DMA((NSEM,)),
     ]
     out_q, out_kv = pl.pallas_call(
         kernel,
-        out_shape=(jax.ShapeDtypeStruct((ROW, PACK, DIM), bf16),
-                   jax.ShapeDtypeStruct((2, ROW, KEYS, DIM), f32)),
+        out_shape=(vmem((ROW, PACK, DIM), bf16), vmem((2, ROW, KEYS, DIM), f32)),
         in_specs=[pl.BlockSpec(memory_space=pl.ANY)] * 6,
         out_specs=[pl.BlockSpec(memory_space=pltpu.VMEM)] * 2,
         scratch_shapes=scratch,
@@ -446,7 +429,7 @@
         out_specs=[pl.BlockSpec(memory_space=pltpu.VMEM)] * 3,
         scratch_shapes=[vmem((TOK, ROW * GRP, DIM), f32)],
         name='relayout',
-    )(out_q, out_kv)
+    )(pltpu.with_memory_space_constraint(out_q, vmem), pltpu.with_memory_space_constraint(out_kv, vmem))
 
 
 def solution(mesh):

time: 43.8 us -> 40.7 us (0.929)
  Pallas kernels: 43 us -> 39.9 us
    pallas_call x1, Pallas kernels: 41.1 us -> 39 us  [call(): pl.pallas_call(kernel, out_shape=(vmem((ROW, PACK, DIM), bf16), vmem((2,...]
    pallas_call x1, Pallas kernels: 1.93 us -> 0.93 us  [call(): pl.pallas_call(relayout, out_shape=(jax.ShapeDtypeStruct(tok, bf16), jax....]
where the time goes in v3:
time: 40.7 us; the launch traced here: 40.6 us
  Pallas kernels  39.9 us (98%)
  between operations  0.64 us (2%)
    pallas_call x1, Pallas kernels, call(): pl.pallas_call(kernel, out_shape=(vmem((ROW, PACK, DIM), bf16), vmem((2,...  39 us
    pallas_call x1, Pallas kernels, call(): pl.pallas_call(relayout, out_shape=(jax.ShapeDtypeStruct(tok, bf16), jax....  0.93 us

profile of v3, /device:TPU:1, one launch (start us, length us, event | category | flops | bytes accessed | tf_op | source)
XLA Modules:
  0.0 40.6 jit_solution(11864150558004294386)
XLA Ops:
  0.6 39.0 %attn_bwd_3d.1 = (bf16[8,48,128]{2,1,0:T(8,128)(2,1)S(1)}, f32[2,8,32,128]{3,2,1,0:T(8,128)S(1)}) custom-call(bf16[2,8,24,128]{3,2,1,0:T(8,128)(2,1)} %q_in.1, bf16[2,8,24,128]{3,2,1,0:T(8,128)(2,1)} %o_in.1, bf16[2,8,24,128]{3,2,1,0:T(8,128)(2,1)} %g_in.1, f32[2,8,24]{2,1,0:T(8,128)} %l_in.1, bf16[32,8,128]{2,1,0:T(8,128)(2,1)} %k_in.1, ...), custom_call_target="tpu_custom_call" | custom-call | tf_op jit(solution)/shard_map/attn_bwd_3d/pallas_call | solution.py:416
  39.6 0.9 %relayout.1 = (bf16[2,8,24,128]{3,2,1,0:T(8,128)(2,1)}, f32[32,8,128]{2,1,0:T(8,128)}, f32[32,8,128]{2,1,0:T(8,128)}) custom-call(bf16[8,48,128]{2,1,0:T(8,128)(2,1)S(1)} %get-tuple-element.5.q_ref, f32[2,8,32,128]{3,2,1,0:T(8,128)S(1)} %get-tuple-element.6.kv_ref), custom_call_target="tpu_custom_call" | custom-call | tf_op jit(solution)/shard_map/relayout/pallas_call | solution.py:425

commit v4 on v0

v4 whole, which is shorter than its diff:
```python
import jax
import jax.numpy as jnp
from jax import lax
from jax.experimental import pallas as pl
from jax.experimental.pallas import tpu as pltpu
from jax.sharding import PartitionSpec as P

CP_AXES = ('cpo', 'cp')
MESH = pl.DeviceIdType.MESH
LOG2E = 1.4426950408889634

ROW = 8
RING = 4
GRP = 3
TOK = 16
KEYS = 32
DIM = 128
QROWS = ROW * GRP * TOK
KROWS = ROW * KEYS
PACK = GRP * TOK
SCALE = DIM ** -0.5
NSEM = 52
NSEND = 10
HOPS = RING

OWN, N1, N2, X = range(4)
GROUPS = (((0, 0), (0, 1), (0, 2), (0, 3)), ((-1, 0), (1, 0), (-1, 1), (1, 3)),
          ((-1, 3), (1, 2), (-1, 2), (1, 1)), ((2, 0), (2, 1), (2, 2), (2, 3)))
PLACE = {chunk: (group, slot) for group, chunks in enumerate(GROUPS) for slot, chunk in enumerate(chunks)}
VIA_PLUS = (2, 0)

NT = (((1,), (1,)), ((), ()))
NN = (((1,), (0,)), ((), ()))
TN = (((0,), (0,)), ((), ()))


def dot(a, b, dims):
    return lax.dot_general(a, b, dims, preferred_element_type=jnp.float32)


def kernel(q_in, o_in, g_in, l_in, k_in, v_in, out_q, out_kv,
           q_vm, o_vm, g_vm, l_vm, k_vm, v_vm, xs, xs2, xk, ts, tt,
           pq, pst, pkv, qd, st, kv, ld, rowc, akv, aqt, oq,
           ra_kv, rb_kv, ra_q, rb_q, fq, in_sem, ssem, rsem):
    me = lax.axis_index('cp')
    cpo = lax.axis_index('cpo')
    z, y = cpo // RING, cpo % RING
    x, core = me // 2, me % 2

    def row_dev(j):
        return (0, cpo, j)

    def ring_devs(axis):
        if axis == 'y':
            return [(0, z * RING + (y + d) % RING, me) for d in (1, 3)]
        return [(0, ((z + d) % RING) * RING + y, me) for d in (1, 3)]

    ydev, zdev = ring_devs('y'), ring_devs('z')

    barrier = pltpu.get_barrier_semaphore()
    for j in range(1, ROW):
        pl.semaphore_signal(barrier, inc=1, device_id=row_dev((me + j) % ROW), device_id_type=MESH)
    for dev in ydev + zdev:
        pl.semaphore_signal(barrier, inc=1, device_id=dev, device_id_type=MESH)

    loads = [pltpu.make_async_copy(src, dst, in_sem.at[i]) for i, (src, dst) in enumerate(
        ((g_in, g_vm), (o_in, o_vm), (q_in, q_vm), (l_in, l_vm), (k_in, k_vm), (v_in, v_vm)))]
    for ld_copy in loads:
        ld_copy.start()

    counter = [0, 0]

    def take(n):
        first = counter[0]
        counter[0] += n
        assert counter[0] <= NSEM
        return first

    def take_send():
        counter[1] += 1
        assert counter[1] <= NSEND
        return counter[1] - 1

    def remote(src, dst, send_i, recv_i, dev):
        return pltpu.make_async_remote_copy(
            src_ref=src, dst_ref=dst, send_sem=ssem.at[send_i], recv_sem=rsem.at[recv_i],
            device_id=dev, device_id_type=MESH)

    def arrived(ref, recv_i):
        remote(ref, ref, 0, recv_i, row_dev(me)).wait_recv()

    sent = []

    def chunk(ref, n, r):
        group, slot = PLACE[n, r]
        return ref.at[group, pl.ds(2 * slot, 2)]

    class Row:
        def __init__(self, src, dst):
            self.dst = dst
            self.recv = take(HOPS)
            send_i = take_send()
            sent.append((send_i, src.at[pl.ds(0, ROW - 1)]))
            for r in (1, 3, 2):
                for c in (0, 1):
                    self.send(src, send_i, r, c)
            self.send(src, send_i, 0, 1 - core)

        def send(self, src, send_i, r, c):
            back = (HOPS - r) % HOPS
            d = (x + r) % HOPS * 2 + c
            remote(src.at[d], self.dst.at[2 * back + core], send_i, self.recv + back, row_dev(d)).start()

        def wait(self, r):
            arrived(self.dst.at[pl.ds(0, 2 if r else 1)], self.recv + r)

    loads[0].wait()
    gf = g_vm[...].reshape(TOK, ROW * GRP, DIM).astype(jnp.float32)
    xs[...] = gf
    for h in range(ROW):
        for g in range(GRP):
            pq[h, GRP + g] = xs[:, h * GRP + g, :].astype(jnp.bfloat16)
    loads[2].wait()
    xs2[...] = q_vm[...].reshape(TOK, ROW * GRP, DIM).astype(jnp.float32)
    for h in range(ROW):
        for g in range(GRP):
            pq[h, g] = xs2[:, h * GRP + g, :].astype(jnp.bfloat16)
    with jax.named_scope('barrier'):
        pl.semaphore_wait(barrier, ROW - 1 + 4)
    row_q = Row(pq, qd.at[OWN])
    qd[OWN, core] = pq[me]

    loads[1].wait()
    delta = jnp.sum(xs[...] * o_vm[...].reshape(TOK, ROW * GRP, DIM).astype(jnp.float32), axis=-1)
    ts[...] = jnp.zeros_like(ts)
    loads[3].wait()
    ts[pl.ds(0, TOK), pl.ds(0, ROW * GRP)] = l_vm[...].reshape(TOK, ROW * GRP)
    ts[pl.ds(TOK, TOK), pl.ds(0, ROW * GRP)] = delta
    tt[...] = ts[...].T
    lane = lax.broadcasted_iota(jnp.int32, (ROW, DIM), 1)
    for which in range(2):
        packed = jnp.zeros((ROW, DIM), jnp.float32)
        for g in range(GRP):
            rows = tt[pl.ds(g, ROW, stride=GRP), :]
            shift = (g * TOK - which * TOK) % DIM
            if shift:
                rows = pltpu.roll(rows, shift, 1)
            packed = jnp.where((lane >= g * TOK) & (lane < (g + 1) * TOK), rows, packed)
        pst[:, which, :] = packed
    row_st = Row(pst, st.at[OWN])
    st[OWN, core] = pst[me]

    loads[4].wait()
    xk[...] = k_vm[...].astype(jnp.float32)
    for h in range(ROW):
        pkv[h, 0] = xk[:, h, :].astype(jnp.bfloat16)
    loads[5].wait()
    xk[...] = v_vm[...].astype(jnp.float32)
    for h in range(ROW):
        pkv[h, 1] = xk[:, h, :].astype(jnp.bfloat16)
    row_kv = Row(pkv, kv.at[OWN])
    kv[OWN, core] = pkv[me]

    class Gather:
        def __init__(self, buf, devs):
            self.buf, self.devs = buf, devs
            self.send_i, first, rest, self.far = take_send(), take(5), take(1), take(1)
            self.recv = {(-1, 0): first, (1, 0): first + 1, (-1, 1): first + 2, (1, 3): first + 3, (1, 2): first + 4}
            self.rest = rest
            sent.append((self.send_i, buf.at[pl.ds(0, RING - 1)]))

        def send(self, r, *sides):
            for side in sides:
                n = 1 if side else -1
                remote(chunk(self.buf, 0, r), chunk(self.buf, n, r), self.send_i, self.recv.get((n, r), self.rest),
                       self.devs[side]).start()

        def wait(self, n, r):
            arrived(chunk(self.buf, n, r), self.recv[n, r])

        def forward(self, n, r):
            self.wait(n, r)
            remote(chunk(self.buf, n, r), chunk(self.buf, 2, r), self.send_i, self.far, self.devs[0 if n < 0 else 1]).start()

        def wait_rest(self):
            arrived(self.buf.at[0, pl.ds(0, 6)], self.rest)

        def wait_far(self):
            arrived(self.buf.at[X], self.far)

    agst, agq, agkv = Gather(st, ydev), Gather(qd, ydev), Gather(kv, zdev)

    def pass_on(row, gather, r):
        row.wait(r)
        if row is row_q:
            pass_on(row_st, agst, r)
        if r == 0:
            gather.send(0, 0, 1)
        elif r == 1:
            gather.send(1, 0)
        elif r == 3:
            gather.send(3, 1, 0)
        else:
            gather.send(2, 1)
            gather.send(1, 1)
            gather.send(2, 0)

    with jax.named_scope('row_0'):
        pass_on(row_q, agq, 0)
        pass_on(row_kv, agkv, 0)

    r_id = lax.broadcasted_iota(jnp.int32, (1, QROWS), 1)
    packet = (r_id * 1366) >> 16
    token = ((r_id >> 3) & 1) * 1024 + (packet & 1) * 8 + (r_id & 7) + (2048 + z * 256)
    for group in range(RING):
        spot = jnp.zeros_like(token)
        for slot, (n, r) in enumerate(GROUPS[group]):
            spot = jnp.where((packet >> 1) == slot, (y + n) % RING * 64 + (x + r) % HOPS * 16, spot)
        rowc[group] = token + spot

    src_id = (3 * lax.broadcasted_iota(jnp.int32, (ROW, DIM), 0)) & 7

    def assemble(group):
        for which in range(2):
            rows = []
            for i in range(ROW):
                rows.append(st[group, pl.ds(3 * i % ROW, 1), which, :])
            rows = pltpu.roll(jnp.concatenate(rows, axis=0), 0, 1, stride=TOK, stride_axis=0)
            for k in range(QROWS // DIM):
                mine = (((lane + k * DIM) * 1366) >> 16) == src_id
                line = jnp.sum(jnp.where(mine, rows, 0.0), axis=0, keepdims=True)
                ld[group, pl.ds(which, 1), pl.ds(k * DIM, DIM)] = line * LOG2E if which == 0 else line

    class Scatter:
        def __init__(self, acc, ra, rb, devs):
            self.acc, self.ra, self.rb, self.devs = acc, ra, rb, devs
            self.send_i, self.first, self.near = take_send(), take(HOPS), take(HOPS)
            sent.append((self.send_i, acc.at[pl.ds(0, RING - 1)]))

        def send_far(self, r):
            side = 0 if r in VIA_PLUS else 1
            remote(chunk(self.acc, 2, r), self.ra.at[r], self.send_i, self.first + r, self.devs[side]).start()

        def send_near(self, side, r):
            remote(chunk(self.acc, -1 if side else 1, r), self.rb.at[side, r], self.send_i, self.near + r, self.devs[side]).start()

        def send_early(self, r):
            self.send_near(1 if r in VIA_PLUS else 0, r)

        def send_late(self, r):
            side = 0 if r in VIA_PLUS else 1
            arrived(self.ra.at[r], self.first + r)
            mine = chunk(self.acc, -1 if side else 1, r)
            mine[...] = mine[...] + self.ra[r]
            self.send_near(side, r)

        def total(self, r):
            arrived(self.rb.at[0, pl.ds(0, 2)], self.near + r)
            return chunk(self.acc, 0, r)[...] + self.rb[0, r] + self.rb[1, r]

    rskv, rsq = Scatter(akv, ra_kv, rb_kv, zdev), Scatter(oq, ra_q, rb_q, ydev)

    band_rows = KROWS // HOPS
    key_row = lax.broadcasted_iota(jnp.int32, (band_rows, QROWS), 0)
    begun = set()

    def add(ref, name, value):
        ref[...] = ref[...] + value if name in begun else value
        begun.add(name)

    def tile(qs, ks):
        with jax.named_scope('tile' + ''.join(map(str, qs)) + 'x' + ''.join(map(str, ks))):
            q = jnp.concatenate([qd[i, :, pl.ds(0, GRP)].reshape(QROWS, DIM) for i in qs], axis=0)
            g = jnp.concatenate([qd[i, :, pl.ds(GRP, GRP)].reshape(QROWS, DIM) for i in qs], axis=0)
            k = jnp.concatenate([kv[i, :, 0].reshape(KROWS, DIM) for i in ks], axis=0)
            v = jnp.concatenate([kv[i, :, 1].reshape(KROWS, DIM) for i in ks], axis=0)
            lse = jnp.concatenate([ld[i, pl.ds(0, 1), :] for i in qs], axis=1)
            dlt = jnp.concatenate([ld[i, pl.ds(1, 1), :] for i in qs], axis=1)
            expo = jnp.exp2(dot(k, q, NT) * (SCALE * LOG2E) - lse)
            bands = []
            for n, r in [at for i in ks for at in GROUPS[i]]:
                first = (z + n) % RING * 1024 + y * 256 + (x + r) % HOPS * band_rows
                seen = jnp.concatenate([key_row <= rowc[i] - first for i in qs], axis=1)
                at = len(bands) * band_rows
                bands.append(jnp.where(seen, expo[at:at + band_rows], 0.0))
            p_t = jnp.concatenate(bands, axis=0)
            dp_t = dot(v, g, NT)
            ds_t = (p_t * (dp_t - dlt)).astype(jnp.bfloat16)
            dv = dot(p_t.astype(jnp.bfloat16), g, NN)
            dk = dot(ds_t, q, NN)
            dq = dot(k, ds_t, TN)
            for n, i in enumerate(ks):
                add(akv.at[i, :, 1], ('v', i), dv[n * KROWS:(n + 1) * KROWS].reshape(ROW, KEYS, DIM))
                add(akv.at[i, :, 0], ('k', i), dk[n * KROWS:(n + 1) * KROWS].reshape(ROW, KEYS, DIM))
            for n, i in enumerate(qs):
                add(aqt.at[i], ('q', i), dq[:, n * QROWS:(n + 1) * QROWS])

    def finish_q(group):
        oq[group] = aqt[group].T.reshape(ROW, PACK, DIM)

    for r in (1, 3, 2):
        with jax.named_scope(f'row_{r}'):
            pass_on(row_q, agq, r)
    for r in (1, 3, 2):
        with jax.named_scope(f'row_kv{r}'):
            pass_on(row_kv, agkv, r)
    assemble(OWN)
    tile([OWN], [OWN])
    def forward_q(n, r):
        agst.forward(n, r)
        agq.forward(n, r)

    with jax.named_scope('fwd_0'):
        forward_q(-1, 0)
        agkv.forward(-1, 0)
    with jax.named_scope('fwd_q1'):
        forward_q(-1, 1)
        forward_q(1, 3)
        agst.wait(1, 0)
        agq.wait(1, 0)
        assemble(N1)
    tile([N1], [OWN])
    with jax.named_scope('fwd_k1'):
        agkv.forward(-1, 1)
        agkv.forward(1, 3)
    with jax.named_scope('fwd_q2'):
        forward_q(1, 2)
    with jax.named_scope('fwd_k2'):
        agkv.forward(1, 2)
        agkv.wait(1, 0)
    tile([OWN, N1], [N1])
    with jax.named_scope('rest_q'):
        agst.wait_rest()
        agq.wait_rest()
        assemble(N2)
    tile([N2], [OWN, N1])
    with jax.named_scope('rest_k'):
        agkv.wait_rest()
    tile([OWN, N1], [N2])
    tile([N2], [N2])
    with jax.named_scope('far_k'):
        agkv.wait_far()
    tile([OWN, N1], [X])
    tile([N2], [X])
    with jax.named_scope('far_q'):
        agst.wait_far()
        agq.wait_far()
        assemble(X)
    tile([X], [X])
    for r in (2, 1, 0, 3):
        rskv.send_far(r)
    tile([X], [N1, N2])
    rskv.send_early(1)
    rskv.send_early(2)
    with jax.named_scope('finish'):
        finish_q(N1)
        finish_q(N2)
    for r in (1, 2, 3, 0):
        rsq.send_early(r)
    tile([X], [OWN])
    finish_q(X)
    for r in (2, 1, 0, 3):
        rsq.send_far(r)
    finish_q(OWN)
    for name, scatter, late, early in (('kv', rskv, (2, 1), (3, 0)), ('q', rsq, (2, 1), ()), ('kv', rskv, (3, 0), ()), ('q', rsq, (3, 0), ())):
        with jax.named_scope(f'late_{name}{late[0]}'):
            for r in late:
                scatter.send_late(r)
        for r in early:
            scatter.send_early(r)

    class Give:
        def __init__(self, src, dst):
            self.src, self.dst = src, dst
            self.send_i, self.recv_i = take_send(), take(1)
            sent.append((self.send_i, src.at[pl.ds(0, ROW - 1)]))

        def send(self, r):
            for c in ((0, 1) if r else (1 - core,)):
                d = (x + r) % HOPS * 2 + c
                remote(self.src.at[2 * r + c], self.dst.at[me], self.send_i, self.recv_i, row_dev(d)).start()

        def wait(self):
            arrived(self.dst.at[pl.ds(0, ROW - 1)], self.recv_i)

    give_kv, give_q = Give(akv.at[OWN], out_kv), Give(fq, out_q)

    def total_kv(r):
        with jax.named_scope(f'total_kv{r}'):
            tot = rskv.total(r)
            akv[OWN, pl.ds(2 * r, 2), 0] = tot[:, 0] * SCALE
            akv[OWN, pl.ds(2 * r, 2), 1] = tot[:, 1]
        give_kv.send(r)

    def total_q(r):
        with jax.named_scope(f'total_q{r}'):
            fq[pl.ds(2 * r, 2)] = (rsq.total(r) * SCALE).astype(jnp.bfloat16)
        give_q.send(r)

    total_kv(2)
    total_kv(1)
    total_q(2)
    total_q(1)
    total_kv(3)
    total_q(3)
    total_q(0)
    total_kv(0)
    out_q[me] = fq[core]
    out_kv[me] = akv[OWN, core]

    with jax.named_scope('final_q'):
        give_q.wait()
    with jax.named_scope('final_kv'):
        give_kv.wait()
    with jax.named_scope('drain'):
        for send_i, ref in sent:
            remote(ref, ref, send_i, 0, row_dev(me)).wait_send()


def relayout(q_ref, kv_ref, dq_ref, dk_ref, dv_ref, rows):
    for h in range(ROW):
        dk_ref[:, h, :] = kv_ref[h, 0]
        dv_ref[:, h, :] = kv_ref[h, 1]
        for g in range(GRP):
            rows[:, h * GRP + g, :] = q_ref[h, pl.ds(g * TOK, TOK), :].astype(jnp.float32)
    dq_ref[...] = rows[...].astype(jnp.bfloat16).reshape(dq_ref.shape)


def call(queries, attn_out, grad_out, log_sum_exp, key_cache, value_cache):
    f32, bf16 = jnp.float32, jnp.bfloat16
    vmem = pltpu.VMEM
    tok = (2, TOK // 2, ROW * GRP, DIM)
    key = (KEYS, ROW, DIM)
    scratch = [
        vmem(tok, bf16), vmem(tok, bf16), vmem(tok, bf16), vmem(tok[:3], f32), vmem(key, bf16), vmem(key, bf16),
        vmem((TOK, ROW * GRP, DIM), f32), vmem((TOK, ROW * GRP, DIM), f32), vmem(key, f32), vmem((DIM, DIM), f32), vmem((DIM, DIM), f32),
        vmem((ROW, 2 * GRP, TOK, DIM), bf16), vmem((ROW, 2, DIM), f32), vmem((ROW, 2, KEYS, DIM), bf16),
        vmem((RING, ROW, 2 * GRP, TOK, DIM), bf16), vmem((RING, ROW, 2, DIM), f32), vmem((RING, ROW, 2, KEYS, DIM), bf16),
        vmem((RING, 8, QROWS), f32), vmem((RING, 1, QROWS), jnp.int32),
        vmem((RING, ROW, 2, KEYS, DIM), f32), vmem((RING, DIM, QROWS), f32), vmem((RING, ROW, PACK, DIM), f32),
        vmem((HOPS, 2, 2, KEYS, DIM), f32), vmem((2, HOPS, 2, 2, KEYS, DIM), f32),
        vmem((HOPS, 2, PACK, DIM), f32), vmem((2, HOPS, 2, PACK, DIM), f32),
        vmem((ROW, PACK, DIM), bf16),
        pltpu.SemaphoreType.DMA((6,)), pltpu.SemaphoreType.DMA((NSEND,)), pltpu.SemaphoreType.DMA((NSEM,)),
    ]
    out_q, out_kv = pl.pallas_call(
        kernel,
        out_shape=(vmem((ROW, PACK, DIM), bf16), vmem((ROW, 2, KEYS, DIM), f32)),
        in_specs=[pl.BlockSpec(memory_space=pl.ANY)] * 6,
        out_specs=[pl.BlockSpec(memory_space=pltpu.VMEM)] * 2,
        scratch_shapes=scratch,
        compiler_params=pltpu.CompilerParams(collective_id=0, has_side_effects=True),
        name='attn_bwd_3d',
    )(queries, attn_out, grad_out, log_sum_exp, key_cache, value_cache)
    return pl.pallas_call(
        relayout,
        out_shape=(jax.ShapeDtypeStruct(tok, bf16), jax.ShapeDtypeStruct(key, f32), jax.ShapeDtypeStruct(key, f32)),
        in_specs=[pl.BlockSpec(memory_space=pltpu.VMEM)] * 2,
        out_specs=[pl.BlockSpec(memory_space=pltpu.VMEM)] * 3,
        scratch_shapes=[vmem((TOK, ROW * GRP, DIM), f32)],
        name='relayout',
    )(pltpu.with_memory_space_constraint(out_q, vmem), pltpu.with_memory_space_constraint(out_kv, vmem))


def solution(mesh):
    row_spec = P(None, CP_AXES, 'heads', None)
    stat_spec = P(None, CP_AXES, 'heads')
    key_spec = P(CP_AXES, 'heads', None)
    return jax.shard_map(call, mesh=mesh, in_specs=(row_spec, row_spec, row_spec, stat_spec, key_spec, key_spec),
                         out_specs=(row_spec, key_spec, key_spec), check_vma=False)
```

time: 756 us -> 38.3 us (0.05)
  waiting for transfers between devices: 554 us -> 0 us
  blocking collectives: 77.5 us -> 0 us
  local copies, waits for them, and re-layouts: 64.5 us -> 0 us
  Pallas kernels: 0 us -> 37.5 us
  matrix products: 33.1 us -> 0 us
  between operations: 14.9 us -> 0.64 us
    reduce_scatter x2 -> x0, waiting for transfers between devices: 399 us -> none  [local_grads(): lax.psum_scatter(dq_part, CP_AXES, scatter_dimension=0, tiled=True)]
    all_gather x4 -> x0, waiting for transfers between devices: 153 us -> none  [the longest x2 125 us: local_grads(): g_all = lax.all_gather(grad_out[slice_idx], CP_AXES, axis=0, tiled=True)]
    all_gather x2 -> x0, blocking collectives: 77.5 us -> none  [local_grads(): stat_all = lax.all_gather(row_stats[slice_idx], CP_AXES, axis=0, tiled=True)]
    pallas_call x0 -> x2, Pallas kernels: none -> 37.5 us  [the longest x1 36.6 us: call(): pl.pallas_call(kernel, out_shape=(vmem((ROW, PACK, DIM), bf16), vmem((ROW...]
    dot_general x10 -> x0, matrix products: 33.1 us -> none  [the longest x2 12 us: block_step(): jnp.einsum('hrgk,khd->rhgd', grad_scores, key_part, preferred_element_typ...]
    reshape x2 -> x0, local copies, waits for them, and re-layouts: 32.8 us -> none  [local_grads(): dq_part = dq_blocks.reshape(slice_len, q_heads, head_dim)]
    all_gather x6 -> x0, local copies, waits for them, and re-layouts: 24 us -> none  [the longest x2 13.5 us: local_grads(): q_all = lax.all_gather(queries[slice_idx], CP_AXES, axis=0, tiled=True)]
  transfers between devices with their start and end apart: 6 -> 0, of which waited for: 5 -> 0; matrix products, arithmetic and copies ran while one was open for 13% -> 0% of each run, Pallas kernels for 0% -> 0%
where the time goes in v4:
time: 38.3 us; the launch traced here: 38.2 us
  Pallas kernels  37.5 us (98%)
  between operations  0.64 us (2%)
    pallas_call x1, Pallas kernels, call(): pl.pallas_call(kernel, out_shape=(vmem((ROW, PACK, DIM), bf16), vmem((ROW...  36.6 us
    pallas_call x1, Pallas kernels, call(): pl.pallas_call(relayout, out_shape=(jax.ShapeDtypeStruct(tok, bf16), jax....  0.93 us

profile of v4, /device:TPU:1, one launch (start us, length us, event | category | flops | bytes accessed | tf_op | source)
XLA Modules:
  0.0 38.2 jit_solution(13313379337230843895)
XLA Ops:
  0.6 36.6 %attn_bwd_3d.1 = (bf16[8,48,128]{2,1,0:T(8,128)(2,1)S(1)}, f32[8,2,32,128]{3,2,1,0:T(8,128)S(1)}) custom-call(bf16[2,8,24,128]{3,2,1,0:T(8,128)(2,1)} %q_in.1, bf16[2,8,24,128]{3,2,1,0:T(8,128)(2,1)} %o_in.1, bf16[2,8,24,128]{3,2,1,0:T(8,128)(2,1)} %g_in.1, f32[2,8,24]{2,1,0:T(8,128)} %l_in.1, bf16[32,8,128]{2,1,0:T(8,128)(2,1)} %k_in.1, ...), custom_call_target="tpu_custom_call" | custom-call | tf_op jit(solution)/shard_map/attn_bwd_3d/pallas_call | solution.py:446
  37.3 0.9 %relayout.1 = (bf16[2,8,24,128]{3,2,1,0:T(8,128)(2,1)}, f32[32,8,128]{2,1,0:T(8,128)}, f32[32,8,128]{2,1,0:T(8,128)}) custom-call(bf16[8,48,128]{2,1,0:T(8,128)(2,1)S(1)} %get-tuple-element.5.q_ref, f32[8,2,32,128]{3,2,1,0:T(8,128)S(1)} %get-tuple-element.6.kv_ref), custom_call_target="tpu_custom_call" | custom-call | tf_op jit(solution)/shard_map/relayout/pallas_call | solution.py:455

commit v5 on v4

--- a/solution.py
+++ b/solution.py
@@ -19,14 +19,15 @@
 KROWS = ROW * KEYS
 PACK = GRP * TOK
 SCALE = DIM ** -0.5
-NSEM = 52
-NSEND = 10
+NSEM = 60
+NSEND = 12
 HOPS = RING
 
 OWN, N1, N2, X = range(4)
 GROUPS = (((0, 0), (0, 1), (0, 2), (0, 3)), ((-1, 0), (1, 0), (-1, 1), (1, 3)),
           ((-1, 3), (1, 2), (-1, 2), (1, 1)), ((2, 0), (2, 1), (2, 2), (2, 3)))
 PLACE = {chunk: (group, slot) for group, chunks in enumerate(GROUPS) for slot, chunk in enumerate(chunks)}
+DIRECT_KV = True
 VIA_PLUS = (2, 0)
 
 NT = (((1,), (1,)), ((), ()))
@@ -52,8 +53,8 @@
 
     def ring_devs(axis):
         if axis == 'y':
-            return [(0, z * RING + (y + d) % RING, me) for d in (1, 3)]
-        return [(0, ((z + d) % RING) * RING + y, me) for d in (1, 3)]
+            return [(0, z * RING + (y + d) % RING, me) for d in (1, 3, 2)]
+        return [(0, ((z + d) % RING) * RING + y, me) for d in (1, 3, 2)]
 
     ydev, zdev = ring_devs('y'), ring_devs('z')
 
@@ -114,66 +115,68 @@
         def wait(self, r):
             arrived(self.dst.at[pl.ds(0, 2 if r else 1)], self.recv + r)
 
-    loads[0].wait()
-    gf = g_vm[...].reshape(TOK, ROW * GRP, DIM).astype(jnp.float32)
-    xs[...] = gf
-    for h in range(ROW):
-        for g in range(GRP):
-            pq[h, GRP + g] = xs[:, h * GRP + g, :].astype(jnp.bfloat16)
-    loads[2].wait()
-    xs2[...] = q_vm[...].reshape(TOK, ROW * GRP, DIM).astype(jnp.float32)
-    for h in range(ROW):
-        for g in range(GRP):
-            pq[h, g] = xs2[:, h * GRP + g, :].astype(jnp.bfloat16)
+    with jax.named_scope('pack_q'):
+        loads[0].wait()
+        gf = g_vm[...].reshape(TOK, ROW * GRP, DIM).astype(jnp.float32)
+        xs[...] = gf
+        for h in range(ROW):
+            for g in range(GRP):
+                pq[h, GRP + g] = xs[:, h * GRP + g, :].astype(jnp.bfloat16)
+        loads[2].wait()
+        xs2[...] = q_vm[...].reshape(TOK, ROW * GRP, DIM).astype(jnp.float32)
+        for h in range(ROW):
+            for g in range(GRP):
+                pq[h, g] = xs2[:, h * GRP + g, :].astype(jnp.bfloat16)
     with jax.named_scope('barrier'):
-        pl.semaphore_wait(barrier, ROW - 1 + 4)
+        pl.semaphore_wait(barrier, ROW - 1 + 6)
     row_q = Row(pq, qd.at[OWN])
     qd[OWN, core] = pq[me]
 
-    loads[1].wait()
-    delta = jnp.sum(xs[...] * o_vm[...].reshape(TOK, ROW * GRP, DIM).astype(jnp.float32), axis=-1)
-    ts[...] = jnp.zeros_like(ts)
-    loads[3].wait()
-    ts[pl.ds(0, TOK), pl.ds(0, ROW * GRP)] = l_vm[...].reshape(TOK, ROW * GRP)
-    ts[pl.ds(TOK, TOK), pl.ds(0, ROW * GRP)] = delta
-    tt[...] = ts[...].T
-    lane = lax.broadcasted_iota(jnp.int32, (ROW, DIM), 1)
-    for which in range(2):
-        packed = jnp.zeros((ROW, DIM), jnp.float32)
-        for g in range(GRP):
-            rows = tt[pl.ds(g, ROW, stride=GRP), :]
-            shift = (g * TOK - which * TOK) % DIM
-            if shift:
-                rows = pltpu.roll(rows, shift, 1)
-            packed = jnp.where((lane >= g * TOK) & (lane < (g + 1) * TOK), rows, packed)
-        pst[:, which, :] = packed
+    with jax.named_scope('stats'):
+        loads[1].wait()
+        delta = jnp.sum(xs[...] * o_vm[...].reshape(TOK, ROW * GRP, DIM).astype(jnp.float32), axis=-1)
+        ts[...] = jnp.zeros_like(ts)
+        loads[3].wait()
+        ts[pl.ds(0, TOK), pl.ds(0, ROW * GRP)] = l_vm[...].reshape(TOK, ROW * GRP)
+        ts[pl.ds(TOK, TOK), pl.ds(0, ROW * GRP)] = delta
+        tt[...] = ts[...].T
+        lane = lax.broadcasted_iota(jnp.int32, (ROW, DIM), 1)
+        for which in range(2):
+            packed = jnp.zeros((ROW, DIM), jnp.float32)
+            for g in range(GRP):
+                rows = tt[pl.ds(g, ROW, stride=GRP), :]
+                shift = (g * TOK - which * TOK) % DIM
+                if shift:
+                    rows = pltpu.roll(rows, shift, 1)
+                packed = jnp.where((lane >= g * TOK) & (lane < (g + 1) * TOK), rows, packed)
+            pst[:, which, :] = packed
     row_st = Row(pst, st.at[OWN])
     st[OWN, core] = pst[me]
 
-    loads[4].wait()
-    xk[...] = k_vm[...].astype(jnp.float32)
-    for h in range(ROW):
-        pkv[h, 0] = xk[:, h, :].astype(jnp.bfloat16)
-    loads[5].wait()
-    xk[...] = v_vm[...].astype(jnp.float32)
-    for h in range(ROW):
-        pkv[h, 1] = xk[:, h, :].astype(jnp.bfloat16)
+    with jax.named_scope('pack_kv'):
+        loads[4].wait()
+        xk[...] = k_vm[...].astype(jnp.float32)
+        for h in range(ROW):
+            pkv[h, 0] = xk[:, h, :].astype(jnp.bfloat16)
+        loads[5].wait()
+        xk[...] = v_vm[...].astype(jnp.float32)
+        for h in range(ROW):
+            pkv[h, 1] = xk[:, h, :].astype(jnp.bfloat16)
     row_kv = Row(pkv, kv.at[OWN])
     kv[OWN, core] = pkv[me]
 
     class Gather:
-        def __init__(self, buf, devs):
-            self.buf, self.devs = buf, devs
-            self.send_i, first, rest, self.far = take_send(), take(5), take(1), take(1)
-            self.recv = {(-1, 0): first, (1, 0): first + 1, (-1, 1): first + 2, (1, 3): first + 3, (1, 2): first + 4}
-            self.rest = rest
+        def __init__(self, buf, devs, direct=False):
+            self.buf, self.devs, self.direct = buf, devs, direct
+            self.recv = {at: take(1) for at in ((-1, 0), (1, 0), (-1, 1), (1, 3)) + (() if direct else ((1, 2),))}
+            self.send_i, self.rest, self.far = take_send(), take(1), take(1)
             sent.append((self.send_i, buf.at[pl.ds(0, RING - 1)]))
 
         def send(self, r, *sides):
             for side in sides:
-                n = 1 if side else -1
-                remote(chunk(self.buf, 0, r), chunk(self.buf, n, r), self.send_i, self.recv.get((n, r), self.rest),
-                       self.devs[side]).start()
+                n = (-1, 1, 2)[side]
+                recv_i = self.far if side == 2 else self.recv.get((n, r), self.rest)
+                remote(chunk(self.buf, 0, r), chunk(self.buf, n, r), self.send_i, recv_i, self.devs[side]).start()
 
         def wait(self, n, r):
             arrived(chunk(self.buf, n, r), self.recv[n, r])
@@ -183,12 +186,12 @@
             remote(chunk(self.buf, n, r), chunk(self.buf, 2, r), self.send_i, self.far, self.devs[0 if n < 0 else 1]).start()
 
         def wait_rest(self):
-            arrived(self.buf.at[0, pl.ds(0, 6)], self.rest)
+            arrived(self.buf.at[0, pl.ds(0, 8 if self.direct else 6)], self.rest)
 
         def wait_far(self):
             arrived(self.buf.at[X], self.far)
 
-    agst, agq, agkv = Gather(st, ydev), Gather(qd, ydev), Gather(kv, zdev)
+    agst, agq, agkv = Gather(st, ydev), Gather(qd, ydev), Gather(kv, zdev, DIRECT_KV)
 
     def pass_on(row, gather, r):
         row.wait(r)
@@ -200,6 +203,10 @@
             gather.send(1, 0)
         elif r == 3:
             gather.send(3, 1, 0)
+        elif gather.direct:
+            gather.send(2, 1, 0)
+            gather.send(1, 1)
+            gather.send(2, 2)
         else:
             gather.send(2, 1)
             gather.send(1, 1)
@@ -258,7 +265,8 @@
             arrived(self.rb.at[0, pl.ds(0, 2)], self.near + r)
             return chunk(self.acc, 0, r)[...] + self.rb[0, r] + self.rb[1, r]
 
-    rskv, rsq = Scatter(akv, ra_kv, rb_kv, zdev), Scatter(oq, ra_q, rb_q, ydev)
+    rsk, rsv = (Scatter(akv.at[i], ra_kv.at[i], rb_kv.at[i], zdev) for i in (0, 1))
+    rsq = Scatter(oq, ra_q, rb_q, ydev)
 
     band_rows = KROWS // HOPS
     key_row = lax.broadcasted_iota(jnp.int32, (band_rows, QROWS), 0)
@@ -290,8 +298,8 @@
             dk = dot(ds_t, q, NN)
             dq = dot(k, ds_t, TN)
             for n, i in enumerate(ks):
-                add(akv.at[i, :, 1], ('v', i), dv[n * KROWS:(n + 1) * KROWS].reshape(ROW, KEYS, DIM))
-                add(akv.at[i, :, 0], ('k', i), dk[n * KROWS:(n + 1) * KROWS].reshape(ROW, KEYS, DIM))
+                add(akv.at[1, i], ('v', i), dv[n * KROWS:(n + 1) * KROWS].reshape(ROW, KEYS, DIM))
+                add(akv.at[0, i], ('k', i), dk[n * KROWS:(n + 1) * KROWS].reshape(ROW, KEYS, DIM))
             for n, i in enumerate(qs):
                 add(aqt.at[i], ('q', i), dq[:, n * QROWS:(n + 1) * QROWS])
 
@@ -326,48 +334,48 @@
     with jax.named_scope('fwd_q2'):
         forward_q(1, 2)
     with jax.named_scope('fwd_k2'):
-        agkv.forward(1, 2)
+        if not DIRECT_KV:
+            agkv.forward(1, 2)
         agkv.wait(1, 0)
     tile([OWN, N1], [N1])
+    with jax.named_scope('rest_k'):
+        agkv.wait_rest()
+    tile([OWN, N1], [N2])
     with jax.named_scope('rest_q'):
         agst.wait_rest()
         agq.wait_rest()
         assemble(N2)
-    tile([N2], [OWN, N1])
-    with jax.named_scope('rest_k'):
-        agkv.wait_rest()
-    tile([OWN, N1], [N2])
-    tile([N2], [N2])
+    tile([N2], [OWN, N1, N2])
     with jax.named_scope('far_k'):
         agkv.wait_far()
-    tile([OWN, N1], [X])
-    tile([N2], [X])
+    tile([OWN, N1, N2], [X])
     with jax.named_scope('far_q'):
         agst.wait_far()
         agq.wait_far()
         assemble(X)
     tile([X], [X])
+    for pair in ((2, 1), (0, 3)):
+        for scatter in (rsv, rsk):
+            for r in pair:
+                scatter.send_far(r)
+    tile([X], [N1, N2, OWN])
+    finish_q(X)
     for r in (2, 1, 0, 3):
-        rskv.send_far(r)
-    tile([X], [N1, N2])
-    rskv.send_early(1)
-    rskv.send_early(2)
+        rsq.send_far(r)
+    for scatter in (rsv, rsk):
+        scatter.send_early(1)
+        scatter.send_early(2)
     with jax.named_scope('finish'):
         finish_q(N1)
         finish_q(N2)
     for r in (1, 2, 3, 0):
         rsq.send_early(r)
-    tile([X], [OWN])
-    finish_q(X)
-    for r in (2, 1, 0, 3):
-        rsq.send_far(r)
     finish_q(OWN)
-    for name, scatter, late, early in (('kv', rskv, (2, 1), (3, 0)), ('q', rsq, (2, 1), ()), ('kv', rskv, (3, 0), ()), ('q', rsq, (3, 0), ())):
-        with jax.named_scope(f'late_{name}{late[0]}'):
-            for r in late:
+
+    def late(name, scatter, *chunks):
+        with jax.named_scope(f'late_{name}{chunks[0]}'):
+            for r in chunks:
                 scatter.send_late(r)
-        for r in early:
-            scatter.send_early(r)
 
     class Give:
         def __init__(self, src, dst):
@@ -383,35 +391,44 @@
         def wait(self):
             arrived(self.dst.at[pl.ds(0, ROW - 1)], self.recv_i)
 
-    give_kv, give_q = Give(akv.at[OWN], out_kv), Give(fq, out_q)
-
-    def total_kv(r):
-        with jax.named_scope(f'total_kv{r}'):
-            tot = rskv.total(r)
-            akv[OWN, pl.ds(2 * r, 2), 0] = tot[:, 0] * SCALE
-            akv[OWN, pl.ds(2 * r, 2), 1] = tot[:, 1]
-        give_kv.send(r)
-
-    def total_q(r):
-        with jax.named_scope(f'total_q{r}'):
-            fq[pl.ds(2 * r, 2)] = (rsq.total(r) * SCALE).astype(jnp.bfloat16)
-        give_q.send(r)
-
-    total_kv(2)
-    total_kv(1)
-    total_q(2)
-    total_q(1)
-    total_kv(3)
-    total_q(3)
-    total_q(0)
-    total_kv(0)
+    give_k, give_v, give_q = Give(akv.at[0, OWN], out_kv.at[0]), Give(akv.at[1, OWN], out_kv.at[1]), Give(fq, out_q)
+
+    def total(name, r):
+        part = pl.ds(2 * r, 2)
+        with jax.named_scope(f'total_{name}{r}'):
+            if name == 'v':
+                akv[1, OWN, part] = rsv.total(r)
+            elif name == 'k':
+                akv[0, OWN, part] = rsk.total(r) * SCALE
+            else:
+                fq[part] = (rsq.total(r) * SCALE).astype(jnp.bfloat16)
+        {'v': give_v, 'k': give_k, 'q': give_q}[name].send(r)
+
+    late('v', rsv, 2, 1)
+    late('k', rsk, 2, 1)
+    rsv.send_early(3)
+    rsk.send_early(3)
+    late('v', rsv, 3)
+    late('k', rsk, 3)
+    late('v', rsv, 0)
+    late('k', rsk, 0)
+    rsv.send_early(0)
+    rsk.send_early(0)
+    late('q', rsq, 2, 1)
+    total('v', 2)
+    total('v', 1)
+    late('q', rsq, 3, 0)
+    for name, r in (('k', 2), ('k', 1), ('v', 3), ('k', 3), ('q', 2), ('q', 1), ('q', 3), ('v', 0), ('k', 0), ('q', 0)):
+        total(name, r)
     out_q[me] = fq[core]
-    out_kv[me] = akv[OWN, core]
+    out_kv[0, me] = akv[0, OWN, core]
+    out_kv[1, me] = akv[1, OWN, core]
 
     with jax.named_scope('final_q'):
         give_q.wait()
     with jax.named_scope('final_kv'):
-        give_kv.wait()
+        give_v.wait()
+        give_k.wait()
     with jax.named_scope('drain'):
         for send_i, ref in sent:
             remote(ref, ref, send_i, 0, row_dev(me)).wait_send()
@@ -419,8 +436,8 @@
 
 def relayout(q_ref, kv_ref, dq_ref, dk_ref, dv_ref, rows):
     for h in range(ROW):
-        dk_ref[:, h, :] = kv_ref[h, 0]
-        dv_ref[:, h, :] = kv_ref[h, 1]
+        dk_ref[:, h, :] = kv_ref[0, h]
+        dv_ref[:, h, :] = kv_ref[1, h]
         for g in range(GRP):
             rows[:, h * GRP + g, :] = q_ref[h, pl.ds(g * TOK, TOK), :].astype(jnp.float32)
     dq_ref[...] = rows[...].astype(jnp.bfloat16).reshape(dq_ref.shape)
@@ -437,15 +454,15 @@
         vmem((ROW, 2 * GRP, TOK, DIM), bf16), vmem((ROW, 2, DIM), f32), vmem((ROW, 2, KEYS, DIM), bf16),
         vmem((RING, ROW, 2 * GRP, TOK, DIM), bf16), vmem((RING, ROW, 2, DIM), f32), vmem((RING, ROW, 2, KEYS, DIM), bf16),
         vmem((RING, 8, QROWS), f32), vmem((RING, 1, QROWS), jnp.int32),
-        vmem((RING, ROW, 2, KEYS, DIM), f32), vmem((RING, DIM, QROWS), f32), vmem((RING, ROW, PACK, DIM), f32),
-        vmem((HOPS, 2, 2, KEYS, DIM), f32), vmem((2, HOPS, 2, 2, KEYS, DIM), f32),
+        vmem((2, RING, ROW, KEYS, DIM), f32), vmem((RING, DIM, QROWS), f32), vmem((RING, ROW, PACK, DIM), f32),
+        vmem((2, HOPS, 2, KEYS, DIM), f32), vmem((2, 2, HOPS, 2, KEYS, DIM), f32),
         vmem((HOPS, 2, PACK, DIM), f32), vmem((2, HOPS, 2, PACK, DIM), f32),
         vmem((ROW, PACK, DIM), bf16),
         pltpu.SemaphoreType.DMA((6,)), pltpu.SemaphoreType.DMA((NSEND,)), pltpu.SemaphoreType.DMA((NSEM,)),
     ]
     out_q, out_kv = pl.pallas_call(
         kernel,
-        out_shape=(vmem((ROW, PACK, DIM), bf16), vmem((ROW, 2, KEYS, DIM), f32)),
+        out_shape=(vmem((ROW, PACK, DIM), bf16), vmem((2, ROW, KEYS, DIM), f32)),
         in_specs=[pl.BlockSpec(memory_space=pl.ANY)] * 6,
         out_specs=[pl.BlockSpec(memory_space=pltpu.VMEM)] * 2,
         scratch_shapes=scratch,

time: 38.3 us -> 38 us (level)
  no operation moved by 1% of the time
where the time goes in v5:
time: 38 us; the launch traced here: 37.8 us
  Pallas kernels  37.2 us (98%)
  between operations  0.64 us (2%)
    pallas_call x1, Pallas kernels, call(): pl.pallas_call(kernel, out_shape=(vmem((ROW, PACK, DIM), bf16), vmem((2,...  36.2 us
    pallas_call x1, Pallas kernels, call(): pl.pallas_call(relayout, out_shape=(jax.ShapeDtypeStruct(tok, bf16), jax....  0.93 us

profile of v5, /device:TPU:1, one launch (start us, length us, event | category | flops | bytes accessed | tf_op | source)
XLA Modules:
  0.0 37.8 jit_solution(5170896664646206571)
XLA Ops:
  0.6 36.2 %attn_bwd_3d.1 = (bf16[8,48,128]{2,1,0:T(8,128)(2,1)S(1)}, f32[2,8,32,128]{3,2,1,0:T(8,128)S(1)}) custom-call(bf16[2,8,24,128]{3,2,1,0:T(8,128)(2,1)} %q_in.1, bf16[2,8,24,128]{3,2,1,0:T(8,128)(2,1)} %o_in.1, bf16[2,8,24,128]{3,2,1,0:T(8,128)(2,1)} %g_in.1, f32[2,8,24]{2,1,0:T(8,128)} %l_in.1, bf16[32,8,128]{2,1,0:T(8,128)(2,1)} %k_in.1, ...), custom_call_target="tpu_custom_call" | custom-call | tf_op jit(solution)/shard_map/attn_bwd_3d/pallas_call | solution.py:463
  36.9 0.9 %relayout.1 = (bf16[2,8,24,128]{3,2,1,0:T(8,128)(2,1)}, f32[32,8,128]{2,1,0:T(8,128)}, f32[32,8,128]{2,1,0:T(8,128)}) custom-call(bf16[8,48,128]{2,1,0:T(8,128)(2,1)S(1)} %get-tuple-element.5.q_ref, f32[2,8,32,128]{3,2,1,0:T(8,128)S(1)} %get-tuple-element.6.kv_ref), custom_call_target="tpu_custom_call" | custom-call | tf_op jit(solution)/shard_map/relayout/pallas_call | solution.py:472

commit v6 on v5

--- a/solution.py
+++ b/solution.py
@@ -40,7 +40,7 @@
 
 
 def kernel(q_in, o_in, g_in, l_in, k_in, v_in, out_q, out_kv,
-           q_vm, o_vm, g_vm, l_vm, k_vm, v_vm, xs, xs2, xk, ts, tt,
+           q_vm, o_vm, g_vm, l_vm, k_vm, v_vm, perm_q, perm_kv, ts, tt,
            pq, pst, pkv, qd, st, kv, ld, rowc, akv, aqt, oq,
            ra_kv, rb_kv, ra_q, rb_q, fq, in_sem, ssem, rsem):
     me = lax.axis_index('cp')
@@ -51,23 +51,30 @@
     def row_dev(j):
         return (0, cpo, j)
 
-    def ring_devs(axis):
-        if axis == 'y':
-            return [(0, z * RING + (y + d) % RING, me) for d in (1, 3, 2)]
-        return [(0, ((z + d) % RING) * RING + y, me) for d in (1, 3, 2)]
-
-    ydev, zdev = ring_devs('y'), ring_devs('z')
+    def along(n, queries):
+        n = n % RING
+        y_step = (core == 0) == queries
+        return jnp.where(y_step, z, (z + n) % RING), jnp.where(y_step, (y + n) % RING, y)
+
+    def ring_devs(queries):
+        devs = []
+        for n in (1, -1, 2):
+            zn, yn = along(n, queries)
+            devs.append((0, zn * RING + yn, me))
+        return devs
+
+    qdev, kdev = ring_devs(True), ring_devs(False)
+
+    loads = [pltpu.make_async_copy(src, dst, in_sem.at[i]) for i, (src, dst) in enumerate(
+        ((g_in, g_vm), (q_in, q_vm), (k_in, k_vm), (v_in, v_vm), (o_in, o_vm), (l_in, l_vm)))]
+    for ld_copy in loads:
+        ld_copy.start()
 
     barrier = pltpu.get_barrier_semaphore()
     for j in range(1, ROW):
         pl.semaphore_signal(barrier, inc=1, device_id=row_dev((me + j) % ROW), device_id_type=MESH)
-    for dev in ydev + zdev:
+    for dev in qdev + kdev:
         pl.semaphore_signal(barrier, inc=1, device_id=dev, device_id_type=MESH)
-
-    loads = [pltpu.make_async_copy(src, dst, in_sem.at[i]) for i, (src, dst) in enumerate(
-        ((g_in, g_vm), (o_in, o_vm), (q_in, q_vm), (l_in, l_vm), (k_in, k_vm), (v_in, v_vm)))]
-    for ld_copy in loads:
-        ld_copy.start()
 
     counter = [0, 0]
 
@@ -115,31 +122,30 @@
         def wait(self, r):
             arrived(self.dst.at[pl.ds(0, 2 if r else 1)], self.recv + r)
 
-    with jax.named_scope('pack_q'):
-        loads[0].wait()
-        gf = g_vm[...].reshape(TOK, ROW * GRP, DIM).astype(jnp.float32)
-        xs[...] = gf
-        for h in range(ROW):
-            for g in range(GRP):
-                pq[h, GRP + g] = xs[:, h * GRP + g, :].astype(jnp.bfloat16)
-        loads[2].wait()
-        xs2[...] = q_vm[...].reshape(TOK, ROW * GRP, DIM).astype(jnp.float32)
-        for h in range(ROW):
-            for g in range(GRP):
-                pq[h, g] = xs2[:, h * GRP + g, :].astype(jnp.bfloat16)
-    with jax.named_scope('barrier'):
-        pl.semaphore_wait(barrier, ROW - 1 + 6)
-    row_q = Row(pq, qd.at[OWN])
-    qd[OWN, core] = pq[me]
-
-    with jax.named_scope('stats'):
-        loads[1].wait()
-        delta = jnp.sum(xs[...] * o_vm[...].reshape(TOK, ROW * GRP, DIM).astype(jnp.float32), axis=-1)
-        ts[...] = jnp.zeros_like(ts)
-        loads[3].wait()
+    def permutation(ref, tokens, heads):
+        n = tokens * heads
+        i = lax.broadcasted_iota(jnp.int32, (n, n), 0)
+        source = (i & (tokens - 1)) * heads + (i >> (tokens.bit_length() - 1))
+        ref[...] = (lax.broadcasted_iota(jnp.int32, (n, n), 1) == source).astype(jnp.float32).astype(jnp.bfloat16)
+
+    permutation(perm_q, TOK, ROW * GRP)
+    permutation(perm_kv, KEYS, ROW)
+    ts[...] = jnp.zeros_like(ts)
+    with jax.named_scope('loads'):
+        for load in loads:
+            load.wait()
+    with jax.named_scope('pack'):
+        prod = g_vm[...].astype(jnp.float32) * o_vm[...].astype(jnp.float32)
+        delta = jnp.sum(prod.reshape(TOK, ROW * GRP, DIM), axis=-1)
         ts[pl.ds(0, TOK), pl.ds(0, ROW * GRP)] = l_vm[...].reshape(TOK, ROW * GRP)
         ts[pl.ds(TOK, TOK), pl.ds(0, ROW * GRP)] = delta
         tt[...] = ts[...].T
+        rows = dot(perm_q[...], jnp.concatenate([q_vm[...], g_vm[...]], axis=1), NN).astype(jnp.bfloat16)
+        for i in (0, 1):
+            pq[:, pl.ds(i * GRP, GRP)] = rows[:, i * DIM:(i + 1) * DIM].reshape(ROW, GRP, TOK, DIM)
+        rows = dot(perm_kv[...], jnp.concatenate([k_vm[...], v_vm[...]], axis=1), NN).astype(jnp.bfloat16)
+        for i in (0, 1):
+            pkv[:, i] = rows[:, i * DIM:(i + 1) * DIM].reshape(ROW, KEYS, DIM)
         lane = lax.broadcasted_iota(jnp.int32, (ROW, DIM), 1)
         for which in range(2):
             packed = jnp.zeros((ROW, DIM), jnp.float32)
@@ -150,18 +156,12 @@
                     rows = pltpu.roll(rows, shift, 1)
                 packed = jnp.where((lane >= g * TOK) & (lane < (g + 1) * TOK), rows, packed)
             pst[:, which, :] = packed
+    with jax.named_scope('barrier'):
+        pl.semaphore_wait(barrier, ROW - 1 + 6)
     row_st = Row(pst, st.at[OWN])
     st[OWN, core] = pst[me]
-
-    with jax.named_scope('pack_kv'):
-        loads[4].wait()
-        xk[...] = k_vm[...].astype(jnp.float32)
-        for h in range(ROW):
-            pkv[h, 0] = xk[:, h, :].astype(jnp.bfloat16)
-        loads[5].wait()
-        xk[...] = v_vm[...].astype(jnp.float32)
-        for h in range(ROW):
-            pkv[h, 1] = xk[:, h, :].astype(jnp.bfloat16)
+    row_q = Row(pq, qd.at[OWN])
+    qd[OWN, core] = pq[me]
     row_kv = Row(pkv, kv.at[OWN])
     kv[OWN, core] = pkv[me]
 
@@ -191,7 +191,7 @@
         def wait_far(self):
             arrived(self.buf.at[X], self.far)
 
-    agst, agq, agkv = Gather(st, ydev), Gather(qd, ydev), Gather(kv, zdev, DIRECT_KV)
+    agst, agq, agkv = Gather(st, qdev), Gather(qd, qdev), Gather(kv, kdev, DIRECT_KV)
 
     def pass_on(row, gather, r):
         row.wait(r)
@@ -218,11 +218,12 @@
 
     r_id = lax.broadcasted_iota(jnp.int32, (1, QROWS), 1)
     packet = (r_id * 1366) >> 16
-    token = ((r_id >> 3) & 1) * 1024 + (packet & 1) * 8 + (r_id & 7) + (2048 + z * 256)
+    token = ((r_id >> 3) & 1) * 1024 + (packet & 1) * 8 + (r_id & 7) + 2048
     for group in range(RING):
         spot = jnp.zeros_like(token)
         for slot, (n, r) in enumerate(GROUPS[group]):
-            spot = jnp.where((packet >> 1) == slot, (y + n) % RING * 64 + (x + r) % HOPS * 16, spot)
+            zq, yq = along(n, True)
+            spot = jnp.where((packet >> 1) == slot, zq * 256 + yq * 64 + (x + r) % HOPS * 16, spot)
         rowc[group] = token + spot
 
     src_id = (3 * lax.broadcasted_iota(jnp.int32, (ROW, DIM), 0)) & 7
@@ -265,8 +266,8 @@
             arrived(self.rb.at[0, pl.ds(0, 2)], self.near + r)
             return chunk(self.acc, 0, r)[...] + self.rb[0, r] + self.rb[1, r]
 
-    rsk, rsv = (Scatter(akv.at[i], ra_kv.at[i], rb_kv.at[i], zdev) for i in (0, 1))
-    rsq = Scatter(oq, ra_q, rb_q, ydev)
+    rsk, rsv = (Scatter(akv.at[i], ra_kv.at[i], rb_kv.at[i], kdev) for i in (0, 1))
+    rsq = Scatter(oq, ra_q, rb_q, qdev)
 
     band_rows = KROWS // HOPS
     key_row = lax.broadcasted_iota(jnp.int32, (band_rows, QROWS), 0)
@@ -287,7 +288,8 @@
             expo = jnp.exp2(dot(k, q, NT) * (SCALE * LOG2E) - lse)
             bands = []
             for n, r in [at for i in ks for at in GROUPS[i]]:
-                first = (z + n) % RING * 1024 + y * 256 + (x + r) % HOPS * band_rows
+                zk, yk = along(n, False)
+                first = zk * 1024 + yk * 256 + (x + r) % HOPS * band_rows
                 seen = jnp.concatenate([key_row <= rowc[i] - first for i in qs], axis=1)
                 at = len(bands) * band_rows
                 bands.append(jnp.where(seen, expo[at:at + band_rows], 0.0))
@@ -338,14 +340,14 @@
             agkv.forward(1, 2)
         agkv.wait(1, 0)
     tile([OWN, N1], [N1])
-    with jax.named_scope('rest_k'):
-        agkv.wait_rest()
-    tile([OWN, N1], [N2])
     with jax.named_scope('rest_q'):
         agst.wait_rest()
         agq.wait_rest()
         assemble(N2)
-    tile([N2], [OWN, N1, N2])
+    tile([N2], [OWN, N1])
+    with jax.named_scope('rest_k'):
+        agkv.wait_rest()
+    tile([OWN, N1, N2], [N2])
     with jax.named_scope('far_k'):
         agkv.wait_far()
     tile([OWN, N1, N2], [X])
@@ -368,8 +370,8 @@
     with jax.named_scope('finish'):
         finish_q(N1)
         finish_q(N2)
-    for r in (1, 2, 3, 0):
-        rsq.send_early(r)
+    rsq.send_early(1)
+    rsq.send_early(2)
     finish_q(OWN)
 
     def late(name, scatter, *chunks):
@@ -410,15 +412,22 @@
     rsk.send_early(3)
     late('v', rsv, 3)
     late('k', rsk, 3)
+    late('q', rsq, 2, 1)
+    rsq.send_early(3)
+    late('q', rsq, 3)
     late('v', rsv, 0)
     late('k', rsk, 0)
     rsv.send_early(0)
     rsk.send_early(0)
-    late('q', rsq, 2, 1)
-    total('v', 2)
-    total('v', 1)
-    late('q', rsq, 3, 0)
-    for name, r in (('k', 2), ('k', 1), ('v', 3), ('k', 3), ('q', 2), ('q', 1), ('q', 3), ('v', 0), ('k', 0), ('q', 0)):
+    late('q', rsq, 0)
+    rsq.send_early(0)
+    for name, r in (('v', 2), ('k', 2), ('v', 1), ('k', 1)):
+        total(name, r)
+    pl.when(core == 0)(lambda: total('q', 2))
+    total('v', 3)
+    total('k', 3)
+    pl.when(core == 1)(lambda: total('q', 2))
+    for name, r in (('q', 1), ('q', 3), ('v', 0), ('k', 0), ('q', 0)):
         total(name, r)
     out_q[me] = fq[core]
     out_kv[0, me] = akv[0, OWN, core]
@@ -448,9 +457,10 @@
     vmem = pltpu.VMEM
     tok = (2, TOK // 2, ROW * GRP, DIM)
     key = (KEYS, ROW, DIM)
+    tok2, key2 = (QROWS, DIM), (KROWS, DIM)
     scratch = [
-        vmem(tok, bf16), vmem(tok, bf16), vmem(tok, bf16), vmem(tok[:3], f32), vmem(key, bf16), vmem(key, bf16),
-        vmem((TOK, ROW * GRP, DIM), f32), vmem((TOK, ROW * GRP, DIM), f32), vmem(key, f32), vmem((DIM, DIM), f32), vmem((DIM, DIM), f32),
+        vmem(tok2, bf16), vmem(tok2, bf16), vmem(tok2, bf16), vmem(tok[:3], f32), vmem(key2, bf16), vmem(key2, bf16),
+        vmem((QROWS, QROWS), bf16), vmem((KROWS, KROWS), bf16), vmem((DIM, DIM), f32), vmem((DIM, DIM), f32),
         vmem((ROW, 2 * GRP, TOK, DIM), bf16), vmem((ROW, 2, DIM), f32), vmem((ROW, 2, KEYS, DIM), bf16),
         vmem((RING, ROW, 2 * GRP, TOK, DIM), bf16), vmem((RING, ROW, 2, DIM), f32), vmem((RING, ROW, 2, KEYS, DIM), bf16),
         vmem((RING, 8, QROWS), f32), vmem((RING, 1, QROWS), jnp.int32),
@@ -468,7 +478,8 @@
         scratch_shapes=scratch,
         compiler_params=pltpu.CompilerParams(collective_id=0, has_side_effects=True),
         name='attn_bwd_3d',
-    )(queries, attn_out, grad_out, log_sum_exp, key_cache, value_cache)
+    )(queries.reshape(tok2), attn_out.reshape(tok2), grad_out.reshape(tok2), log_sum_exp,
+      key_cache.reshape(key2), value_cache.reshape(key2))
     return pl.pallas_call(
         relayout,
         out_shape=(jax.ShapeDtypeStruct(tok, bf16), jax.ShapeDtypeStruct(key, f32), jax.ShapeDtypeStruct(key, f32)),

time: 38 us -> 37.5 us (0.987)
  Pallas kernels: 37.2 us -> 36.7 us
    pallas_call x1, Pallas kernels: 36.2 us -> 35.8 us  [call(): pl.pallas_call(kernel, out_shape=(vmem((ROW, PACK, DIM), bf16), vmem((2,...]
where the time goes in v6:
time: 37.5 us; the launch traced here: 37.3 us
  Pallas kernels  36.7 us (98%)
  between operations  0.64 us (2%)
    pallas_call x1, Pallas kernels, call(): pl.pallas_call(kernel, out_shape=(vmem((ROW, PACK, DIM), bf16), vmem((2,...  35.8 us
    pallas_call x1, Pallas kernels, call(): pl.pallas_call(relayout, out_shape=(jax.ShapeDtypeStruct(tok, bf16), jax....  0.93 us

profile of v6, /device:TPU:1, one launch (start us, length us, event | category | flops | bytes accessed | tf_op | source)
XLA Modules:
  0.0 37.3 jit_solution(18238847011757020340)
XLA Ops:
  0.6 35.8 %attn_bwd_3d.1 = (bf16[8,48,128]{2,1,0:T(8,128)(2,1)S(1)}, f32[2,8,32,128]{3,2,1,0:T(8,128)S(1)}) custom-call(bf16[384,128]{1,0:T(8,128)(2,1)} %bitcast.5, bf16[384,128]{1,0:T(8,128)(2,1)} %bitcast.6, bf16[384,128]{1,0:T(8,128)(2,1)} %bitcast.7, f32[2,8,24]{2,1,0:T(8,128)} %l_in.1, bf16[256,128]{1,0:T(8,128)(2,1)} %bitcast.8, bf16[256,128]{1,0:T(8,128)(2,1)} %bitcast.9), custom_call_target="tpu_custom_call" | custom-call | tf_op jit(solution)/shard_map/attn_bwd_3d/pallas_call | solution.py:473
  36.4 0.9 %relayout.1 = (bf16[2,8,24,128]{3,2,1,0:T(8,128)(2,1)}, f32[32,8,128]{2,1,0:T(8,128)}, f32[32,8,128]{2,1,0:T(8,128)}) custom-call(bf16[8,48,128]{2,1,0:T(8,128)(2,1)S(1)} %get-tuple-element.5.q_ref, f32[2,8,32,128]{3,2,1,0:T(8,128)S(1)} %get-tuple-element.6.kv_ref), custom_call_target="tpu_custom_call" | custom-call | tf_op jit(solution)/shard_map/relayout/pallas_call | solution.py:483

commit v7 on v6

--- a/solution.py
+++ b/solution.py
@@ -106,18 +106,15 @@
     class Row:
         def __init__(self, src, dst):
             self.dst = dst
-            self.recv = take(HOPS)
-            send_i = take_send()
-            sent.append((send_i, src.at[pl.ds(0, ROW - 1)]))
-            for r in (1, 3, 2):
-                for c in (0, 1):
-                    self.send(src, send_i, r, c)
-            self.send(src, send_i, 0, 1 - core)
-
-        def send(self, src, send_i, r, c):
-            back = (HOPS - r) % HOPS
-            d = (x + r) % HOPS * 2 + c
-            remote(src.at[d], self.dst.at[2 * back + core], send_i, self.recv + back, row_dev(d)).start()
+            self.src, self.recv, self.send_i = src, take(HOPS), take_send()
+            sent.append((self.send_i, src.at[pl.ds(0, ROW - 1)]))
+
+        def send(self, *chips):
+            for r in chips:
+                back = (HOPS - r) % HOPS
+                for c in ((0, 1) if r else (1 - core,)):
+                    d = (x + r) % HOPS * 2 + c
+                    remote(self.src.at[d], self.dst.at[2 * back + core], self.send_i, self.recv + back, row_dev(d)).start()
 
         def wait(self, r):
             arrived(self.dst.at[pl.ds(0, 2 if r else 1)], self.recv + r)
@@ -158,11 +155,16 @@
             pst[:, which, :] = packed
     with jax.named_scope('barrier'):
         pl.semaphore_wait(barrier, ROW - 1 + 6)
-    row_st = Row(pst, st.at[OWN])
+    row_st, row_q, row_kv = Row(pst, st.at[OWN]), Row(pq, qd.at[OWN]), Row(pkv, kv.at[OWN])
+    for row in (row_st, row_q, row_kv):
+        row.send(0)
+    row_st.send(1, 3, 2)
+    row_q.send(1, 3)
+    row_kv.send(1, 3)
+    row_q.send(2)
+    row_kv.send(2)
     st[OWN, core] = pst[me]
-    row_q = Row(pq, qd.at[OWN])
     qd[OWN, core] = pq[me]
-    row_kv = Row(pkv, kv.at[OWN])
     kv[OWN, core] = pkv[me]
 
     class Gather:
@@ -308,12 +310,11 @@
     def finish_q(group):
         oq[group] = aqt[group].T.reshape(ROW, PACK, DIM)
 
-    for r in (1, 3, 2):
-        with jax.named_scope(f'row_{r}'):
-            pass_on(row_q, agq, r)
-    for r in (1, 3, 2):
-        with jax.named_scope(f'row_kv{r}'):
-            pass_on(row_kv, agkv, r)
+    for chips in ((1, 3), (2,)):
+        for name, row, gather in (('', row_q, agq), ('kv', row_kv, agkv)):
+            for r in chips:
+                with jax.named_scope(f'row_{name}{r}'):
+                    pass_on(row, gather, r)
     assemble(OWN)
     tile([OWN], [OWN])
     def forward_q(n, r):
@@ -340,14 +341,14 @@
             agkv.forward(1, 2)
         agkv.wait(1, 0)
     tile([OWN, N1], [N1])
+    with jax.named_scope('rest_k'):
+        agkv.wait_rest()
+    tile([OWN, N1], [N2])
     with jax.named_scope('rest_q'):
         agst.wait_rest()
         agq.wait_rest()
         assemble(N2)
-    tile([N2], [OWN, N1])
-    with jax.named_scope('rest_k'):
-        agkv.wait_rest()
-    tile([OWN, N1, N2], [N2])
+    tile([N2], [OWN, N1, N2])
     with jax.named_scope('far_k'):
         agkv.wait_far()
     tile([OWN, N1, N2], [X])
@@ -362,16 +363,26 @@
                 scatter.send_far(r)
     tile([X], [N1, N2, OWN])
     finish_q(X)
-    for r in (2, 1, 0, 3):
-        rsq.send_far(r)
+    rsq.send_far(2)
+    rsq.send_far(1)
+
+    @pl.when(core == 0)
+    def _():
+        rsq.send_far(0)
+        rsq.send_far(3)
+
     for scatter in (rsv, rsk):
         scatter.send_early(1)
         scatter.send_early(2)
     with jax.named_scope('finish'):
         finish_q(N1)
         finish_q(N2)
-    rsq.send_early(1)
-    rsq.send_early(2)
+
+    @pl.when(core == 0)
+    def _():
+        rsq.send_early(1)
+        rsq.send_early(2)
+
     finish_q(OWN)
 
     def late(name, scatter, *chunks):
@@ -406,29 +417,59 @@
                 fq[part] = (rsq.total(r) * SCALE).astype(jnp.bfloat16)
         {'v': give_v, 'k': give_k, 'q': give_q}[name].send(r)
 
+    def early(r):
+        rsv.send_early(r)
+        rsk.send_early(r)
+
+    def totals(names, *chunks):
+        for r in chunks:
+            for name in names:
+                total(name, r)
+
     late('v', rsv, 2, 1)
     late('k', rsk, 2, 1)
-    rsv.send_early(3)
-    rsk.send_early(3)
-    late('v', rsv, 3)
-    late('k', rsk, 3)
-    late('q', rsq, 2, 1)
-    rsq.send_early(3)
-    late('q', rsq, 3)
-    late('v', rsv, 0)
-    late('k', rsk, 0)
-    rsv.send_early(0)
-    rsk.send_early(0)
-    late('q', rsq, 0)
-    rsq.send_early(0)
-    for name, r in (('v', 2), ('k', 2), ('v', 1), ('k', 1)):
-        total(name, r)
-    pl.when(core == 0)(lambda: total('q', 2))
-    total('v', 3)
-    total('k', 3)
-    pl.when(core == 1)(lambda: total('q', 2))
-    for name, r in (('q', 1), ('q', 3), ('v', 0), ('k', 0), ('q', 0)):
-        total(name, r)
+
+    @pl.when(core == 0)
+    def _():
+        early(3)
+        late('v', rsv, 3)
+        late('k', rsk, 3)
+        late('q', rsq, 2, 1)
+        rsq.send_early(3)
+        late('q', rsq, 3)
+        late('v', rsv, 0)
+        late('k', rsk, 0)
+        early(0)
+        late('q', rsq, 0)
+        rsq.send_early(0)
+        totals('vk', 2, 1)
+        totals('q', 2)
+        totals('vk', 3)
+        totals('q', 1, 3)
+        totals('vkq', 0)
+
+    @pl.when(core == 1)
+    def _():
+        rsq.send_far(0)
+        rsq.send_far(3)
+        rsq.send_early(1)
+        rsq.send_early(2)
+        early(3)
+        late('v', rsv, 3)
+        late('k', rsk, 3)
+        late('q', rsq, 2, 1)
+        totals('vk', 2, 1)
+        rsq.send_early(3)
+        late('q', rsq, 3)
+        late('v', rsv, 0)
+        late('k', rsk, 0)
+        early(0)
+        totals('vk', 3)
+        late('q', rsq, 0)
+        rsq.send_early(0)
+        totals('q', 2, 1, 3)
+        totals('vkq', 0)
+
     out_q[me] = fq[core]
     out_kv[0, me] = akv[0, OWN, core]
     out_kv[1, me] = akv[1, OWN, core]

time: 37.5 us -> 36.5 us (0.973)
  Pallas kernels: 36.7 us -> 35.8 us
    pallas_call x1, Pallas kernels: 35.8 us -> 34.8 us  [call(): pl.pallas_call(kernel, out_shape=(vmem((ROW, PACK, DIM), bf16), vmem((2,...]
where the time goes in v7:
time: 36.5 us; the launch traced here: 36.4 us
  Pallas kernels  35.8 us (98%)
  between operations  0.64 us (2%)
    pallas_call x1, Pallas kernels, call(): pl.pallas_call(kernel, out_shape=(vmem((ROW, PACK, DIM), bf16), vmem((2,...  34.8 us
    pallas_call x1, Pallas kernels, call(): pl.pallas_call(relayout, out_shape=(jax.ShapeDtypeStruct(tok, bf16), jax....  0.93 us

profile of v7, /device:TPU:1, one launch (start us, length us, event | category | flops | bytes accessed | tf_op | source)
XLA Modules:
  0.0 36.4 jit_solution(11324406588112751344)
XLA Ops:
  0.6 34.8 %attn_bwd_3d.1 = (bf16[8,48,128]{2,1,0:T(8,128)(2,1)S(1)}, f32[2,8,32,128]{3,2,1,0:T(8,128)S(1)}) custom-call(bf16[384,128]{1,0:T(8,128)(2,1)} %bitcast.5, bf16[384,128]{1,0:T(8,128)(2,1)} %bitcast.6, bf16[384,128]{1,0:T(8,128)(2,1)} %bitcast.7, f32[2,8,24]{2,1,0:T(8,128)} %l_in.1, bf16[256,128]{1,0:T(8,128)(2,1)} %bitcast.8, bf16[256,128]{1,0:T(8,128)(2,1)} %bitcast.9), custom_call_target="tpu_custom_call" | custom-call | tf_op jit(solution)/shard_map/attn_bwd_3d/pallas_call | solution.py:514
  35.5 0.9 %relayout.1 = (bf16[2,8,24,128]{3,2,1,0:T(8,128)(2,1)}, f32[32,8,128]{2,1,0:T(8,128)}, f32[32,8,128]{2,1,0:T(8,128)}) custom-call(bf16[8,48,128]{2,1,0:T(8,128)(2,1)S(1)} %get-tuple-element.5.q_ref, f32[2,8,32,128]{3,2,1,0:T(8,128)S(1)} %get-tuple-element.6.kv_ref), custom_call_target="tpu_custom_call" | custom-call | tf_op jit(solution)/shard_map/relayout/pallas_call | solution.py:524

commit v8 on v7

--- a/solution.py
+++ b/solution.py
@@ -19,8 +19,6 @@
 KROWS = ROW * KEYS
 PACK = GRP * TOK
 SCALE = DIM ** -0.5
-NSEM = 60
-NSEND = 12
 HOPS = RING
 
 OWN, N1, N2, X = range(4)
@@ -30,6 +28,10 @@
 DIRECT_KV = True
 VIA_PLUS = (2, 0)
 
+NSEM = 48
+LINE_Q, LINE_KV, LINE_DQ = 50, 32, 24
+SENT = (ROW - 1 + (RING - 1) * ROW) * (LINE_Q + LINE_KV) + (RING - 1) * ROW * (2 * KEYS + PACK) + (ROW - 1) * (2 * KEYS + LINE_DQ)
+
 NT = (((1,), (1,)), ((), ()))
 NN = (((1,), (0,)), ((), ()))
 TN = (((0,), (0,)), ((), ()))
@@ -42,7 +44,7 @@
 def kernel(q_in, o_in, g_in, l_in, k_in, v_in, out_q, out_kv,
            q_vm, o_vm, g_vm, l_vm, k_vm, v_vm, perm_q, perm_kv, ts, tt,
            pq, pst, pkv, qd, st, kv, ld, rowc, akv, aqt, oq,
-           ra_kv, rb_kv, ra_q, rb_q, fq, in_sem, ssem, rsem):
+           ra_kv, rb_kv, ra_q, rb_q, fq, in_sem, ssem, rsem, gauge):
     me = lax.axis_index('cp')
     cpo = lax.axis_index('cpo')
     z, y = cpo // RING, cpo % RING
@@ -65,7 +67,7 @@
 
     qdev, kdev = ring_devs(True), ring_devs(False)
 
-    loads = [pltpu.make_async_copy(src, dst, in_sem.at[i]) for i, (src, dst) in enumerate(
+    loads = [pltpu.make_async_copy(src, dst, in_sem.at[i // 5]) for i, (src, dst) in enumerate(
         ((g_in, g_vm), (q_in, q_vm), (k_in, k_vm), (v_in, v_vm), (o_in, o_vm), (l_in, l_vm)))]
     for ld_copy in loads:
         ld_copy.start()
@@ -76,7 +78,7 @@
     for dev in qdev + kdev:
         pl.semaphore_signal(barrier, inc=1, device_id=dev, device_id_type=MESH)
 
-    counter = [0, 0]
+    counter = [0]
 
     def take(n):
         first = counter[0]
@@ -84,40 +86,35 @@
         assert counter[0] <= NSEM
         return first
 
-    def take_send():
-        counter[1] += 1
-        assert counter[1] <= NSEND
-        return counter[1] - 1
-
-    def remote(src, dst, send_i, recv_i, dev):
+    def remote(src, dst, recv_i, dev):
         return pltpu.make_async_remote_copy(
-            src_ref=src, dst_ref=dst, send_sem=ssem.at[send_i], recv_sem=rsem.at[recv_i],
+            src_ref=src, dst_ref=dst, send_sem=ssem.at[0], recv_sem=rsem.at[recv_i],
             device_id=dev, device_id_type=MESH)
 
-    def arrived(ref, recv_i):
-        remote(ref, ref, 0, recv_i, row_dev(me)).wait_recv()
-
-    sent = []
+    def lines(n):
+        return gauge.at[pl.ds(0, n)]
+
+    def arrived(n, recv_i):
+        remote(lines(n), lines(n), recv_i, row_dev(me)).wait_recv()
 
     def chunk(ref, n, r):
         group, slot = PLACE[n, r]
         return ref.at[group, pl.ds(2 * slot, 2)]
 
     class Row:
-        def __init__(self, src, dst):
-            self.dst = dst
-            self.src, self.recv, self.send_i = src, take(HOPS), take_send()
-            sent.append((self.send_i, src.at[pl.ds(0, ROW - 1)]))
+        def __init__(self, size, *pairs):
+            self.size, self.pairs, self.recv = size, pairs, take(HOPS)
 
         def send(self, *chips):
             for r in chips:
                 back = (HOPS - r) % HOPS
                 for c in ((0, 1) if r else (1 - core,)):
                     d = (x + r) % HOPS * 2 + c
-                    remote(self.src.at[d], self.dst.at[2 * back + core], self.send_i, self.recv + back, row_dev(d)).start()
+                    for src, dst in self.pairs:
+                        remote(src.at[d], dst.at[2 * back + core], self.recv + back, row_dev(d)).start()
 
         def wait(self, r):
-            arrived(self.dst.at[pl.ds(0, 2 if r else 1)], self.recv + r)
+            arrived(self.size * (2 if r else 1), self.recv + r)
 
     def permutation(ref, tokens, heads):
         n = tokens * heads
@@ -129,8 +126,9 @@
     permutation(perm_kv, KEYS, ROW)
     ts[...] = jnp.zeros_like(ts)
     with jax.named_scope('loads'):
-        for load in loads:
-            load.wait()
+        whole = lines((3 * QROWS + 2 * KROWS) // 2)
+        pltpu.make_async_copy(whole, whole, in_sem.at[0]).wait()
+        loads[5].wait()
     with jax.named_scope('pack'):
         prod = g_vm[...].astype(jnp.float32) * o_vm[...].astype(jnp.float32)
         delta = jnp.sum(prod.reshape(TOK, ROW * GRP, DIM), axis=-1)
@@ -155,10 +153,10 @@
             pst[:, which, :] = packed
     with jax.named_scope('barrier'):
         pl.semaphore_wait(barrier, ROW - 1 + 6)
-    row_st, row_q, row_kv = Row(pst, st.at[OWN]), Row(pq, qd.at[OWN]), Row(pkv, kv.at[OWN])
-    for row in (row_st, row_q, row_kv):
-        row.send(0)
-    row_st.send(1, 3, 2)
+    row_q = Row(LINE_Q, (pst, st.at[OWN]), (pq, qd.at[OWN]))
+    row_kv = Row(LINE_KV, (pkv, kv.at[OWN]))
+    row_q.send(0)
+    row_kv.send(0)
     row_q.send(1, 3)
     row_kv.send(1, 3)
     row_q.send(2)
@@ -168,37 +166,36 @@
     kv[OWN, core] = pkv[me]
 
     class Gather:
-        def __init__(self, buf, devs, direct=False):
-            self.buf, self.devs, self.direct = buf, devs, direct
+        def __init__(self, size, bufs, devs, direct=False):
+            self.size, self.bufs, self.devs, self.direct = 2 * size, bufs, devs, direct
             self.recv = {at: take(1) for at in ((-1, 0), (1, 0), (-1, 1), (1, 3)) + (() if direct else ((1, 2),))}
-            self.send_i, self.rest, self.far = take_send(), take(1), take(1)
-            sent.append((self.send_i, buf.at[pl.ds(0, RING - 1)]))
+            self.rest, self.far = take(1), take(1)
 
         def send(self, r, *sides):
             for side in sides:
                 n = (-1, 1, 2)[side]
                 recv_i = self.far if side == 2 else self.recv.get((n, r), self.rest)
-                remote(chunk(self.buf, 0, r), chunk(self.buf, n, r), self.send_i, recv_i, self.devs[side]).start()
+                for buf in self.bufs:
+                    remote(chunk(buf, 0, r), chunk(buf, n, r), recv_i, self.devs[side]).start()
 
         def wait(self, n, r):
-            arrived(chunk(self.buf, n, r), self.recv[n, r])
+            arrived(self.size, self.recv[n, r])
 
         def forward(self, n, r):
             self.wait(n, r)
-            remote(chunk(self.buf, n, r), chunk(self.buf, 2, r), self.send_i, self.far, self.devs[0 if n < 0 else 1]).start()
+            for buf in self.bufs:
+                remote(chunk(buf, n, r), chunk(buf, 2, r), self.far, self.devs[0 if n < 0 else 1]).start()
 
         def wait_rest(self):
-            arrived(self.buf.at[0, pl.ds(0, 8 if self.direct else 6)], self.rest)
+            arrived(self.size * (4 if self.direct else 3), self.rest)
 
         def wait_far(self):
-            arrived(self.buf.at[X], self.far)
-
-    agst, agq, agkv = Gather(st, qdev), Gather(qd, qdev), Gather(kv, kdev, DIRECT_KV)
+            arrived(self.size * HOPS, self.far)
+
+    agq, agkv = Gather(LINE_Q, (st, qd), qdev), Gather(LINE_KV, (kv,), kdev, DIRECT_KV)
 
     def pass_on(row, gather, r):
         row.wait(r)
-        if row is row_q:
-            pass_on(row_st, agst, r)
         if r == 0:
             gather.send(0, 0, 1)
         elif r == 1:
@@ -242,34 +239,33 @@
                 ld[group, pl.ds(which, 1), pl.ds(k * DIM, DIM)] = line * LOG2E if which == 0 else line
 
     class Scatter:
-        def __init__(self, acc, ra, rb, devs):
-            self.acc, self.ra, self.rb, self.devs = acc, ra, rb, devs
-            self.send_i, self.first, self.near = take_send(), take(HOPS), take(HOPS)
-            sent.append((self.send_i, acc.at[pl.ds(0, RING - 1)]))
+        def __init__(self, size, acc, ra, rb, devs):
+            self.size, self.acc, self.ra, self.rb, self.devs = 2 * size, acc, ra, rb, devs
+            self.first, self.near = take(HOPS), take(HOPS)
 
         def send_far(self, r):
             side = 0 if r in VIA_PLUS else 1
-            remote(chunk(self.acc, 2, r), self.ra.at[r], self.send_i, self.first + r, self.devs[side]).start()
+            remote(chunk(self.acc, 2, r), self.ra.at[r], self.first + r, self.devs[side]).start()
 
         def send_near(self, side, r):
-            remote(chunk(self.acc, -1 if side else 1, r), self.rb.at[side, r], self.send_i, self.near + r, self.devs[side]).start()
+            remote(chunk(self.acc, -1 if side else 1, r), self.rb.at[side, r], self.near + r, self.devs[side]).start()
 
         def send_early(self, r):
             self.send_near(1 if r in VIA_PLUS else 0, r)
 
         def send_late(self, r):
             side = 0 if r in VIA_PLUS else 1
-            arrived(self.ra.at[r], self.first + r)
+            arrived(self.size, self.first + r)
             mine = chunk(self.acc, -1 if side else 1, r)
             mine[...] = mine[...] + self.ra[r]
             self.send_near(side, r)
 
         def total(self, r):
-            arrived(self.rb.at[0, pl.ds(0, 2)], self.near + r)
+            arrived(2 * self.size, self.near + r)
             return chunk(self.acc, 0, r)[...] + self.rb[0, r] + self.rb[1, r]
 
-    rsk, rsv = (Scatter(akv.at[i], ra_kv.at[i], rb_kv.at[i], kdev) for i in (0, 1))
-    rsq = Scatter(oq, ra_q, rb_q, qdev)
+    rsk, rsv = (Scatter(KEYS, akv.at[i], ra_kv.at[i], rb_kv.at[i], kdev) for i in (0, 1))
+    rsq = Scatter(PACK, oq, ra_q, rb_q, qdev)
 
     band_rows = KROWS // HOPS
     key_row = lax.broadcasted_iota(jnp.int32, (band_rows, QROWS), 0)
@@ -317,17 +313,12 @@
                     pass_on(row, gather, r)
     assemble(OWN)
     tile([OWN], [OWN])
-    def forward_q(n, r):
-        agst.forward(n, r)
-        agq.forward(n, r)
-
     with jax.named_scope('fwd_0'):
-        forward_q(-1, 0)
+        agq.forward(-1, 0)
         agkv.forward(-1, 0)
     with jax.named_scope('fwd_q1'):
-        forward_q(-1, 1)
-        forward_q(1, 3)
-        agst.wait(1, 0)
+        agq.forward(-1, 1)
+        agq.forward(1, 3)
         agq.wait(1, 0)
         assemble(N1)
     tile([N1], [OWN])
@@ -335,7 +326,7 @@
         agkv.forward(-1, 1)
         agkv.forward(1, 3)
     with jax.named_scope('fwd_q2'):
-        forward_q(1, 2)
+        agq.forward(1, 2)
     with jax.named_scope('fwd_k2'):
         if not DIRECT_KV:
             agkv.forward(1, 2)
@@ -345,7 +336,6 @@
         agkv.wait_rest()
     tile([OWN, N1], [N2])
     with jax.named_scope('rest_q'):
-        agst.wait_rest()
         agq.wait_rest()
         assemble(N2)
     tile([N2], [OWN, N1, N2])
@@ -353,7 +343,6 @@
         agkv.wait_far()
     tile([OWN, N1, N2], [X])
     with jax.named_scope('far_q'):
-        agst.wait_far()
         agq.wait_far()
         assemble(X)
     tile([X], [X])
@@ -391,20 +380,18 @@
                 scatter.send_late(r)
 
     class Give:
-        def __init__(self, src, dst):
-            self.src, self.dst = src, dst
-            self.send_i, self.recv_i = take_send(), take(1)
-            sent.append((self.send_i, src.at[pl.ds(0, ROW - 1)]))
+        def __init__(self, size, src, dst):
+            self.size, self.src, self.dst, self.recv_i = size, src, dst, take(1)
 
         def send(self, r):
             for c in ((0, 1) if r else (1 - core,)):
                 d = (x + r) % HOPS * 2 + c
-                remote(self.src.at[2 * r + c], self.dst.at[me], self.send_i, self.recv_i, row_dev(d)).start()
+                remote(self.src.at[2 * r + c], self.dst.at[me], self.recv_i, row_dev(d)).start()
 
         def wait(self):
-            arrived(self.dst.at[pl.ds(0, ROW - 1)], self.recv_i)
-
-    give_k, give_v, give_q = Give(akv.at[0, OWN], out_kv.at[0]), Give(akv.at[1, OWN], out_kv.at[1]), Give(fq, out_q)
+            arrived(self.size * (ROW - 1), self.recv_i)
+
+    give_k, give_v, give_q = Give(KEYS, akv.at[0, OWN], out_kv.at[0]), Give(KEYS, akv.at[1, OWN], out_kv.at[1]), Give(LINE_DQ, fq, out_q)
 
     def total(name, r):
         part = pl.ds(2 * r, 2)
@@ -454,10 +441,10 @@
         rsq.send_far(3)
         rsq.send_early(1)
         rsq.send_early(2)
+        late('q', rsq, 2, 1)
         early(3)
         late('v', rsv, 3)
         late('k', rsk, 3)
-        late('q', rsq, 2, 1)
         totals('vk', 2, 1)
         rsq.send_early(3)
         late('q', rsq, 3)
@@ -480,8 +467,7 @@
         give_v.wait()
         give_k.wait()
     with jax.named_scope('drain'):
-        for send_i, ref in sent:
-            remote(ref, ref, send_i, 0, row_dev(me)).wait_send()
+        remote(lines(SENT), lines(SENT), 0, row_dev(me)).wait_send()
 
 
 def relayout(q_ref, kv_ref, dq_ref, dk_ref, dv_ref, rows):
@@ -509,7 +495,8 @@
         vmem((2, HOPS, 2, KEYS, DIM), f32), vmem((2, 2, HOPS, 2, KEYS, DIM), f32),
         vmem((HOPS, 2, PACK, DIM), f32), vmem((2, HOPS, 2, PACK, DIM), f32),
         vmem((ROW, PACK, DIM), bf16),
-        pltpu.SemaphoreType.DMA((6,)), pltpu.SemaphoreType.DMA((NSEND,)), pltpu.SemaphoreType.DMA((NSEM,)),
+        pltpu.SemaphoreType.DMA((2,)), pltpu.SemaphoreType.DMA((1,)), pltpu.SemaphoreType.DMA((NSEM,)),
+        vmem((SENT, DIM), f32),
     ]
     out_q, out_kv = pl.pallas_call(
         kernel,

time: 36.5 us -> 36.4 us (level)
  no operation moved by 1% of the time
where the time goes in v8:
time: 36.4 us; the launch traced here: 36.2 us
  Pallas kernels  35.6 us (98%)
  between operations  0.64 us (2%)
    pallas_call x1, Pallas kernels, call(): pl.pallas_call(kernel, out_shape=(vmem((ROW, PACK, DIM), bf16), vmem((2,...  34.7 us
    pallas_call x1, Pallas kernels, call(): pl.pallas_call(relayout, out_shape=(jax.ShapeDtypeStruct(tok, bf16), jax....  0.93 us

profile of v8, /device:TPU:1, one launch (start us, length us, event | category | flops | bytes accessed | tf_op | source)
XLA Modules:
  0.0 36.2 jit_solution(13150787774266588078)
XLA Ops:
  0.6 34.7 %attn_bwd_3d.1 = (bf16[8,48,128]{2,1,0:T(8,128)(2,1)S(1)}, f32[2,8,32,128]{3,2,1,0:T(8,128)S(1)}) custom-call(bf16[384,128]{1,0:T(8,128)(2,1)} %bitcast.5, bf16[384,128]{1,0:T(8,128)(2,1)} %bitcast.6, bf16[384,128]{1,0:T(8,128)(2,1)} %bitcast.7, f32[2,8,24]{2,1,0:T(8,128)} %l_in.1, bf16[256,128]{1,0:T(8,128)(2,1)} %bitcast.8, bf16[256,128]{1,0:T(8,128)(2,1)} %bitcast.9), custom_call_target="tpu_custom_call" | custom-call | tf_op jit(solution)/shard_map/attn_bwd_3d/pallas_call | solution.py:501
  35.3 0.9 %relayout.1 = (bf16[2,8,24,128]{3,2,1,0:T(8,128)(2,1)}, f32[32,8,128]{2,1,0:T(8,128)}, f32[32,8,128]{2,1,0:T(8,128)}) custom-call(bf16[8,48,128]{2,1,0:T(8,128)(2,1)S(1)} %get-tuple-element.5.q_ref, f32[2,8,32,128]{3,2,1,0:T(8,128)S(1)} %get-tuple-element.6.kv_ref), custom_call_target="tpu_custom_call" | custom-call | tf_op jit(solution)/shard_map/relayout/pallas_call | solution.py:511

commit v9 on v8

--- a/solution.py
+++ b/solution.py
@@ -157,8 +157,10 @@
     row_kv = Row(LINE_KV, (pkv, kv.at[OWN]))
     row_q.send(0)
     row_kv.send(0)
-    row_q.send(1, 3)
-    row_kv.send(1, 3)
+    row_q.send(1)
+    row_kv.send(1)
+    row_q.send(3)
+    row_kv.send(3)
     row_q.send(2)
     row_kv.send(2)
     st[OWN, core] = pst[me]
@@ -306,11 +308,10 @@
     def finish_q(group):
         oq[group] = aqt[group].T.reshape(ROW, PACK, DIM)
 
-    for chips in ((1, 3), (2,)):
+    for r in (1, 3, 2):
         for name, row, gather in (('', row_q, agq), ('kv', row_kv, agkv)):
-            for r in chips:
-                with jax.named_scope(f'row_{name}{r}'):
-                    pass_on(row, gather, r)
+            with jax.named_scope(f'row_{name}{r}'):
+                pass_on(row, gather, r)
     assemble(OWN)
     tile([OWN], [OWN])
     with jax.named_scope('fwd_0'):
@@ -429,10 +430,8 @@
         early(0)
         late('q', rsq, 0)
         rsq.send_early(0)
-        totals('vk', 2, 1)
-        totals('q', 2)
-        totals('vk', 3)
-        totals('q', 1, 3)
+        totals('vk', 2, 1, 3)
+        totals('q', 2, 1, 3)
         totals('vkq', 0)
 
     @pl.when(core == 1)
@@ -441,17 +440,17 @@
         rsq.send_far(3)
         rsq.send_early(1)
         rsq.send_early(2)
-        late('q', rsq, 2, 1)
         early(3)
         late('v', rsv, 3)
         late('k', rsk, 3)
+        late('q', rsq, 2, 1)
+        rsq.send_early(3)
         totals('vk', 2, 1)
-        rsq.send_early(3)
         late('q', rsq, 3)
+        totals('vk', 3)
         late('v', rsv, 0)
         late('k', rsk, 0)
         early(0)
-        totals('vk', 3)
         late('q', rsq, 0)
         rsq.send_early(0)
         totals('q', 2, 1, 3)

time: 36.4 us -> 36.2 us (level)
  no operation moved by 1% of the time
where the time goes in v9:
time: 36.2 us; the launch traced here: 36 us
  Pallas kernels  35.4 us (98%)
  between operations  0.64 us (2%)
    pallas_call x1, Pallas kernels, call(): pl.pallas_call(kernel, out_shape=(vmem((ROW, PACK, DIM), bf16), vmem((2,...  34.5 us
    pallas_call x1, Pallas kernels, call(): pl.pallas_call(relayout, out_shape=(jax.ShapeDtypeStruct(tok, bf16), jax....  0.93 us

profile of v9, /device:TPU:1, one launch (start us, length us, event | category | flops | bytes accessed | tf_op | source)
XLA Modules:
  0.0 36.0 jit_solution(14323467895506616205)
XLA Ops:
  0.6 34.5 %attn_bwd_3d.1 = (bf16[8,48,128]{2,1,0:T(8,128)(2,1)S(1)}, f32[2,8,32,128]{3,2,1,0:T(8,128)S(1)}) custom-call(bf16[384,128]{1,0:T(8,128)(2,1)} %bitcast.5, bf16[384,128]{1,0:T(8,128)(2,1)} %bitcast.6, bf16[384,128]{1,0:T(8,128)(2,1)} %bitcast.7, f32[2,8,24]{2,1,0:T(8,128)} %l_in.1, bf16[256,128]{1,0:T(8,128)(2,1)} %bitcast.8, bf16[256,128]{1,0:T(8,128)(2,1)} %bitcast.9), custom_call_target="tpu_custom_call" | custom-call | tf_op jit(solution)/shard_map/attn_bwd_3d/pallas_call | solution.py:500
  35.1 0.9 %relayout.1 = (bf16[2,8,24,128]{3,2,1,0:T(8,128)(2,1)}, f32[32,8,128]{2,1,0:T(8,128)}, f32[32,8,128]{2,1,0:T(8,128)}) custom-call(bf16[8,48,128]{2,1,0:T(8,128)(2,1)S(1)} %get-tuple-element.5.q_ref, f32[2,8,32,128]{3,2,1,0:T(8,128)S(1)} %get-tuple-element.6.kv_ref), custom_call_target="tpu_custom_call" | custom-call | tf_op jit(solution)/shard_map/relayout/pallas_call | solution.py:510

commit v10 on v9

--- a/solution.py
+++ b/solution.py
@@ -157,10 +157,10 @@
     row_kv = Row(LINE_KV, (pkv, kv.at[OWN]))
     row_q.send(0)
     row_kv.send(0)
+    row_q.send(3)
+    row_kv.send(3)
     row_q.send(1)
     row_kv.send(1)
-    row_q.send(3)
-    row_kv.send(3)
     row_q.send(2)
     row_kv.send(2)
     st[OWN, core] = pst[me]

time: 36.2 us -> 36.2 us (level)
  no operation moved by 1% of the time
where the time goes in v10:
time: 36.2 us; the launch traced here: 36 us
  Pallas kernels  35.4 us (98%)
  between operations  0.64 us (2%)
    pallas_call x1, Pallas kernels, call(): pl.pallas_call(kernel, out_shape=(vmem((ROW, PACK, DIM), bf16), vmem((2,...  34.5 us
    pallas_call x1, Pallas kernels, call(): pl.pallas_call(relayout, out_shape=(jax.ShapeDtypeStruct(tok, bf16), jax....  0.93 us

profile of v10, /device:TPU:1, one launch (start us, length us, event | category | flops | bytes accessed | tf_op | source)
XLA Modules:
  0.0 36.0 jit_solution(7586779972356309895)
XLA Ops:
  0.6 34.5 %attn_bwd_3d.1 = (bf16[8,48,128]{2,1,0:T(8,128)(2,1)S(1)}, f32[2,8,32,128]{3,2,1,0:T(8,128)S(1)}) custom-call(bf16[384,128]{1,0:T(8,128)(2,1)} %bitcast.5, bf16[384,128]{1,0:T(8,128)(2,1)} %bitcast.6, bf16[384,128]{1,0:T(8,128)(2,1)} %bitcast.7, f32[2,8,24]{2,1,0:T(8,128)} %l_in.1, bf16[256,128]{1,0:T(8,128)(2,1)} %bitcast.8, bf16[256,128]{1,0:T(8,128)(2,1)} %bitcast.9), custom_call_target="tpu_custom_call" | custom-call | tf_op jit(solution)/shard_map/attn_bwd_3d/pallas_call | solution.py:500
  35.1 0.9 %relayout.1 = (bf16[2,8,24,128]{3,2,1,0:T(8,128)(2,1)}, f32[32,8,128]{2,1,0:T(8,128)}, f32[32,8,128]{2,1,0:T(8,128)}) custom-call(bf16[8,48,128]{2,1,0:T(8,128)(2,1)S(1)} %get-tuple-element.5.q_ref, f32[2,8,32,128]{3,2,1,0:T(8,128)S(1)} %get-tuple-element.6.kv_ref), custom_call_target="tpu_custom_call" | custom-call | tf_op jit(solution)/shard_map/relayout/pallas_call | solution.py:510

commit v11 on v9

--- a/solution.py
+++ b/solution.py
@@ -425,12 +425,13 @@
         late('q', rsq, 2, 1)
         rsq.send_early(3)
         late('q', rsq, 3)
+        late('q', rsq, 0)
+        rsq.send_early(0)
+        totals('vk', 2)
         late('v', rsv, 0)
         late('k', rsk, 0)
         early(0)
-        late('q', rsq, 0)
-        rsq.send_early(0)
-        totals('vk', 2, 1, 3)
+        totals('vk', 1, 3)
         totals('q', 2, 1, 3)
         totals('vkq', 0)
 

time: 36.2 us -> 36.2 us (level)
  no operation moved by 1% of the time
where the time goes in v11:
time: 36.2 us; the launch traced here: 36 us
  Pallas kernels  35.4 us (98%)
  between operations  0.64 us (2%)
    pallas_call x1, Pallas kernels, call(): pl.pallas_call(kernel, out_shape=(vmem((ROW, PACK, DIM), bf16), vmem((2,...  34.5 us
    pallas_call x1, Pallas kernels, call(): pl.pallas_call(relayout, out_shape=(jax.ShapeDtypeStruct(tok, bf16), jax....  0.93 us

profile of v11, /device:TPU:1, one launch (start us, length us, event | category | flops | bytes accessed | tf_op | source)
XLA Modules:
  0.0 36.0 jit_solution(10354046807442034055)
XLA Ops:
  0.6 34.5 %attn_bwd_3d.1 = (bf16[8,48,128]{2,1,0:T(8,128)(2,1)S(1)}, f32[2,8,32,128]{3,2,1,0:T(8,128)S(1)}) custom-call(bf16[384,128]{1,0:T(8,128)(2,1)} %bitcast.5, bf16[384,128]{1,0:T(8,128)(2,1)} %bitcast.6, bf16[384,128]{1,0:T(8,128)(2,1)} %bitcast.7, f32[2,8,24]{2,1,0:T(8,128)} %l_in.1, bf16[256,128]{1,0:T(8,128)(2,1)} %bitcast.8, bf16[256,128]{1,0:T(8,128)(2,1)} %bitcast.9), custom_call_target="tpu_custom_call" | custom-call | tf_op jit(solution)/shard_map/attn_bwd_3d/pallas_call | solution.py:501
  35.1 0.9 %relayout.1 = (bf16[2,8,24,128]{3,2,1,0:T(8,128)(2,1)}, f32[32,8,128]{2,1,0:T(8,128)}, f32[32,8,128]{2,1,0:T(8,128)}) custom-call(bf16[8,48,128]{2,1,0:T(8,128)(2,1)S(1)} %get-tuple-element.5.q_ref, f32[2,8,32,128]{3,2,1,0:T(8,128)S(1)} %get-tuple-element.6.kv_ref), custom_call_target="tpu_custom_call" | custom-call | tf_op jit(solution)/shard_map/relayout/pallas_call | solution.py:511
